TPU v7x, 32 devices: a 4x4x1 block of a 4x4x8 slice. The times are simulated.
32 devices in a mesh: rep: 1 (over z), dp: 32 (over x, y, core).
Axes of the slice: x: 4, y: 4, z: 1, core: 2. Of those that a mesh axis runs over, the one named last changes fastest.
The devices are a block of a 4x4x8 slice.
Arguments:
- x: bfloat16 [32, 2048, 1280], P(('rep', 'dp'))
- dy: bfloat16 [32, 2048, 1280], P(('rep', 'dp'))
- w_gate: bfloat16 [2, 1280, 4480], replicated
- w_up: bfloat16 [2, 1280, 4480], replicated
- w_down: bfloat16 [2, 4480, 1280], replicated
- m_w_gate: float32 [2, 1280, 4480], P(None, 'dp')
- m_w_up: float32 [2, 1280, 4480], P(None, 'dp')
- m_w_down: float32 [2, 4480, 1280], P(None, 'dp')
- v_w_gate: float32 [2, 1280, 4480], P(None, 'dp')
- v_w_up: float32 [2, 1280, 4480], P(None, 'dp')
- v_w_down: float32 [2, 4480, 1280], P(None, 'dp')
Outputs:
- output 1: bfloat16 [2, 1280, 4480], P('rep')
- output 2: bfloat16 [2, 1280, 4480], P('rep')
- output 3: bfloat16 [2, 4480, 1280], P('rep')
- output 4: float32 [2, 1280, 4480], P('rep', 'dp')
- output 5: float32 [2, 1280, 4480], P('rep', 'dp')
- output 6: float32 [2, 4480, 1280], P('rep', 'dp')
- output 7: float32 [2, 1280, 4480], P('rep', 'dp')
- output 8: float32 [2, 1280, 4480], P('rep', 'dp')
- output 9: float32 [2, 4480, 1280], P('rep', 'dp')
All inputs are finite; a program needn't handle non-finite values.
Results may differ from a plain program's by a relative error of at most 0.022.
Values are sent between devices in bfloat16 or wider.
A program may use at most 768 MiB of HBM per device.

v0:
```python
import jax
import jax.numpy as jnp
from jax import lax

NAMES = ("w_gate", "w_up", "w_down")


def matmul(a, w):
    return jnp.dot(a, w, preferred_element_type=jnp.float32).astype(jnp.bfloat16)


def normed(h):
    wide = h.astype(jnp.float32)
    scale = lax.rsqrt(jnp.mean(wide**2, -1, keepdims=True) + 1e-6)
    return (wide * scale).astype(jnp.bfloat16)


def layer(h, w):
    a = normed(h)
    gate = jnp.dot(a, w["w_gate"], preferred_element_type=jnp.float32)
    up = jnp.dot(a, w["w_up"], preferred_element_type=jnp.float32)
    return h + matmul((jax.nn.silu(gate) * up).astype(jnp.bfloat16), w["w_down"])


def adamw(w, m, v, g):
    m = 0.9 * m + 0.1 * g
    v = 0.95 * v + 0.05 * g * g
    step = m * lax.rsqrt(v + 1e-8) + 0.1 * w
    return (w - 0.02 * step).astype(jnp.bfloat16), m, v


def clipped(gradients, sum_of_squares, count):
    factor = jnp.minimum(1.0, 0.5 * lax.rsqrt(sum_of_squares / count + 1e-30))
    return [g * factor for g in gradients]


def stack(weights, h):
    for number in range(weights["w_gate"].shape[0]):
        h = layer(h, {name: w[number] for name, w in weights.items()})
    return h


def solution(mesh):
    groups = mesh.shape["rep"]

    def step(x, dy, *arrays):
        weights, m, v = (arrays[i : i + 3] for i in (0, 3, 6))
        x, dy = (t.reshape(groups, -1, *t.shape[1:]) for t in (x, dy))

        def of_a_group(x, dy):
            _, back = jax.vjp(lambda w: stack(w, x), dict(zip(NAMES, weights, strict=True)))
            by_weights = back(dy)[0]
            gradients = [by_weights[name].astype(jnp.float32) for name in NAMES]
            gradients = clipped(gradients, sum(jnp.sum(g * g) for g in gradients), sum(g.size for g in gradients))
            new = [adamw(w.astype(jnp.float32), m, v, g) for w, m, v, g in zip(weights, m, v, gradients, strict=True)]
            return tuple(one[which] for which in range(3) for one in new)

        return tuple(t.reshape(-1, *t.shape[2:]) for t in jax.vmap(of_a_group)(x, dy))

    return step
```

profile of v0, /device:TPU:97, one launch (start us, length us, event | category | flops | bytes accessed | tf_op | source)
XLA Modules:
  0.0 1486.7 jit_solution(14672069611661788730)
XLA Ops:
  7.3 3.6 fusion.55
  10.8 8.0 copy.6
  18.8 32.0 %fusion.49 = f32[2048,4480]{1,0:T(8,128)} fusion(bf16[2,1280,4480]{2,1,0:T(8,128)(2,1)} %param, bf16[1,2048,1280]{2,1,0:T(8,128)(2,1)} %param.4, f32[2048]{0:T(1024)S(1)} %add_rsqrt_fusion), kind=kOutput, calls=%fused_computation.64 | convolution fusion | flops 23495966720 | bytes 53420032 | tf_op jit(solution)/vmap(jvp())/dot_general | solution.py:20
  50.9 30.0 %fusion.47 = f32[2048,4480]{1,0:T(8,128)} fusion(bf16[2,1280,4480]{2,1,0:T(8,128)(2,1)} %param.5, bf16[1,2048,1280]{2,1,0:T(8,128)(2,1)S(1)} %bitcast.358, f32[2048]{0:T(1024)S(1)} %add_rsqrt_fusion), kind=kOutput, calls=%fused_computation.62 | convolution fusion | flops 23495966720 | bytes 53420032 | tf_op jit(solution)/vmap(jvp())/dot_general | solution.py:21
  80.9 30.6 %fusion.28 = bf16[2048,4480]{1,0:T(8,128)(2,1)} fusion(f32[2048,4480]{1,0:T(8,128)} %fusion.47, f32[2048,4480]{1,0:T(8,128)} %fusion.49), kind=kLoop, calls=%fused_computation.37 | loop fusion | flops 55050240 | bytes 91750400
  111.5 33.2 %fusion.59 = (f32[2048]{0:T(1024)S(1)}, bf16[1,2048,1280]{1,2,0:T(8,128)(2,1)}) fusion(bf16[1,2048,1280]{1,2,0:T(8,128)(2,1)} %copy.6, bf16[2048,4480]{1,0:T(8,128)(2,1)} %fusion.28, bf16[2,4480,1280]{2,1,0:T(8,128)(2,1)} %param.3), kind=kOutput, calls=%fused_computation.74 | convolution fusion | flops 23501207552 | bytes 40312832 | tf_op jit(solution)/vmap(jvp())/dot_general | solution.py:9
  145.3 32.2 %fusion.37 = f32[2048,4480]{1,0:T(8,128)} fusion(bf16[2,1280,4480]{2,1,0:T(8,128)(2,1)} %param, bf16[1,2048,1280]{1,2,0:T(8,128)(2,1)} %get-tuple-element.28, f32[2048]{0:T(1024)S(1)} %bitcast.364), kind=kOutput, calls=%fused_computation.52 | convolution fusion | flops 23495966720 | bytes 53420032 | tf_op jit(solution)/vmap(jvp())/dot_general | solution.py:20
  177.5 30.7 %fusion.41 = f32[2048,4480]{1,0:T(8,128)} fusion(bf16[2,1280,4480]{2,1,0:T(8,128)(2,1)} %param.5, bf16[1,2048,1280]{1,2,0:T(8,128)(2,1)S(1)} %copy-done.1, f32[2048]{0:T(1024)S(1)} %bitcast.365), kind=kOutput, calls=%fused_computation.56 | convolution fusion | flops 23495966720 | bytes 53420032 | tf_op jit(solution)/vmap(jvp())/dot_general | solution.py:21
  208.2 30.5 %convolution_convert_fusion.1 = bf16[2048,4480]{1,0:T(8,128)(2,1)} fusion(bf16[2,4480,1280]{2,1,0:T(8,128)(2,1)} %param.3, bf16[1,2048,1280]{2,1,0:T(8,128)(2,1)S(1)} %bitcast.360), kind=kOutput, calls=%fused_computation.36 | convolution fusion | flops 23497277440 | bytes 35061760 | tf_op jit(solution)/vmap(transpose(jvp()))/dot_general | solution.py:9
  238.7 7.9 copy.7
  246.6 36.1 %fusion.8 = bf16[2048,4480]{1,0:T(8,128)(2,1)} fusion(f32[2048,4480]{1,0:T(8,128)} %fusion.37, f32[2048,4480]{1,0:T(8,128)} %fusion.41, bf16[2048,4480]{1,0:T(8,128)(2,1)} %convolution_convert_fusion.1), kind=kLoop, calls=%fused_computation.11 | loop fusion | flops 110100480 | bytes 110100480
  282.7 32.0 %fusion.73 = bf16[2048,1280]{0,1:T(8,128)(2,1)} fusion(bf16[2048,4480]{1,0:T(8,128)(2,1)} %fusion.8, bf16[2,1280,4480]{2,1,0:T(8,128)(2,1)} %param), kind=kOutput, calls=%fused_computation.84 | convolution fusion | flops 23488102400 | bytes 35061760 | tf_op jit(solution)/vmap(transpose(jvp()))/dot_general | solution.py:20
  314.7 36.9 %fusion.61 = (f32[2048]{0:T(1024)S(1)}, bf16[1,2048,1280]{1,2,0:T(8,128)(2,1)}) fusion(bf16[1,2048,1280]{1,2,0:T(8,128)(2,1)} %get-tuple-element.28, bf16[2048,1280]{0,1:T(8,128)(2,1)} %fusion.73, bf16[2,1280,4480]{2,1,0:T(8,128)(2,1)} %param.5, bf16[2048,4480]{1,0:T(8,128)(2,1)} %convolution_convert_fusion.1, f32[2048,4480]{1,0:T(8,128)} %fusion.37), kind=kOutput, calls=%fused_computation.76 | convolution fusion | flops 23558879232 | bytes 82255872 | tf_op jit(solution)/vmap(transpose(jvp()))/dot_general | solution.py:21
  351.7 12.3 fusion.97
  364.0 31.5 %convolution_convert_fusion = bf16[2048,4480]{1,0:T(8,128)(2,1)} fusion(bf16[2048,1280]{0,1:T(8,128)(2,1)} %fusion.97, bf16[2,4480,1280]{2,1,0:T(8,128)(2,1)} %param.3), kind=kOutput, calls=%fused_computation.35 | convolution fusion | flops 23497277440 | bytes 35061760 | tf_op jit(solution)/vmap(transpose(jvp()))/dot_general | solution.py:9
  395.5 38.9 %fusion.4 = f32[4480,1280]{0,1:T(8,128)} fusion(bf16[2048,4480]{1,0:T(8,128)(2,1)} %convolution_convert_fusion, f32[2048,4480]{1,0:T(8,128)} %fusion.49, bf16[1,2048,1280]{2,1,0:T(8,128)(2,1)} %param.4, f32[2048]{0:T(1024)S(1)} %copy-done.14), kind=kOutput, calls=%fused_computation.8 | convolution fusion | flops 23551016960 | bytes 83238912 | tf_op jit(solution)/vmap(transpose(jvp()))/dot_general | solution.py:21
  435.1 38.0 %fusion.24 = f32[4480,1280]{0,1:T(8,128)} fusion(bf16[2048,4480]{1,0:T(8,128)(2,1)} %convolution_convert_fusion.1, f32[2048,4480]{1,0:T(8,128)} %fusion.37, bf16[1,2048,1280]{1,2,0:T(8,128)(2,1)} %get-tuple-element.28, f32[2048]{0:T(1024)S(1)} %bitcast.367), kind=kOutput, calls=%fused_computation.33 | convolution fusion | flops 23551016960 | bytes 83238912 | tf_op jit(solution)/vmap(transpose(jvp()))/dot_general | solution.py:21
  473.3 47.7 %fusion.12 = f32[4480,1280]{0,1:T(8,128)} fusion(f32[2048,4480]{1,0:T(8,128)} %fusion.49, f32[2048,4480]{1,0:T(8,128)} %fusion.47, bf16[2048,4480]{1,0:T(8,128)(2,1)} %convolution_convert_fusion, bf16[1,2048,1280]{2,1,0:T(8,128)(2,1)} %param.4, f32[2048]{0:T(1024)S(1)} %copy-done.14), kind=kOutput, calls=%fused_computation.15 | convolution fusion | flops 23596892160 | bytes 119939072 | tf_op jit(solution)/vmap(transpose(jvp()))/dot_general | solution.py:20
  521.1 30.8 %fusion.102 = f32[4480,1280]{0,1:T(8,128)} fusion(bf16[2048,4480]{1,0:T(8,128)(2,1)} %fusion.8, bf16[1,2048,1280]{1,2,0:T(8,128)(2,1)} %get-tuple-element.28, f32[2048]{0:T(1024)S(1)} %bitcast.368), kind=kOutput, calls=%fused_computation.96 | convolution fusion | flops 23495966720 | bytes 46538752 | tf_op jit(solution)/vmap(transpose(jvp()))/dot_general | solution.py:20
  552.1 41.3 %fusion.30 = f32[4480,1280]{1,0:T(8,128)} fusion(f32[2048,4480]{1,0:T(8,128)} %fusion.41, f32[2048,4480]{1,0:T(8,128)} %fusion.37, bf16[1,2048,1280]{2,1,0:T(8,128)(2,1)} %param.2), kind=kOutput, calls=%fused_computation.39 | convolution fusion | flops 23543152640 | bytes 101580800 | tf_op jit(solution)/vmap(transpose(jvp()))/dot_general | solution.py:9
  593.4 179.5 %fusion = f32[144,1280]{1,0:T(8,128)S(1)} fusion(f32[4480,1280]{1,0:T(8,128)} %fusion.30), kind=kCustom, calls=%all-reduce-scatter | all-reduce-scatter fusion | flops 5898241 | bytes 23674880
  773.0 4.4 collective-permute-start
  777.5 31.1 %fusion.150 = f32[1280,4480]{0,1:T(8,128)} fusion(bf16[2048,1280]{0,1:T(8,128)(2,1)} %fusion.97, bf16[2048,4480]{1,0:T(8,128)(2,1)} %fusion.28), kind=kOutput, calls=%fused_computation.166 | convolution fusion | flops 23488102400 | bytes 46530560 | tf_op jit(solution)/vmap(transpose(jvp()))/dot_general | solution.py:9
  808.5 179.7 %fusion.1 = f32[1280,144]{0,1:T(8,128)S(1)} fusion(f32[1280,4480]{0,1:T(8,128)} %fusion.150), kind=kCustom, calls=%all-reduce-scatter.1 | all-reduce-scatter fusion | flops 5898241 | bytes 23674880
  988.3 4.4 collective-permute-start.1
  992.7 1.0 concatenate
  993.8 3.0 collective-permute-done.1
  998.6 1.0 fusion.110
  999.7 1.1 convert_bitcast_fusion.3
  1000.9 1.3 convert_bitcast_fusion.4
  1003.1 13.2 reduce-scatter.25.cloned.1.call-done
  1016.4 1.1 convert_bitcast_fusion.5
  1017.5 129.9 %reduce-scatter.23.cloned.1.call-done = f32[4480,40]{0,1:T(8,128)} async-done(((f32[4480,1280]{0,1:T(8,128)}), f32[4480,40]{0,1:T(8,128)}) %reduce-scatter.23.cloned.1.call-update) | async-done | bytes 716816
  1147.4 1.1 convert_bitcast_fusion.6
  1151.5 45.3 %all-reduce.16 = f32[]{:T(128)} all-reduce(f32[]{:T(128)S(6)} %add.114), channel_id=5, replica_groups=mesh['rep'=1,'dp'=32] {'dp'}, use_global_device_ids=true, to_apply=%region_3.4.clone | all-reduce | flops 1 | bytes 8 | tf_op jit(solution)/vmap()/reduce_sum | solution.py:54
  1197.5 3.1 fusion.138
  1200.6 1.4 copy.10
  1202.2 4.8 fusion.135
  1207.4 4.7 fusion.136
  1212.2 2.2 copy.12
  1214.4 2.2 copy.13
  1216.6 65.2 %all-gather.14.cloned.1.call-done = bf16[1,2,4480,1280]{3,1,0,2:T(2,128)(2,1)} async-done(((bf16[1,2,140,1280]{3,1,0,2:T(2,128)(2,1)}), bf16[1,2,4480,1280]{3,1,0,2:T(2,128)(2,1)}) %all-gather.14.cloned.1.call-update) | async-done | bytes 22937616 | tf_op jit(solution)/reshape | solution.py:58
  1281.7 22.7 %copy.11 = bf16[2,4480,1280]{2,1,0:T(8,128)(2,1)} copy(bf16[2,4480,1280]{2,0,1:T(2,128)(2,1)} %bitcast.354) | data formatting | bytes 45875200
  1304.4 60.7 %all-gather.12.cloned.1.call-done = bf16[1,2,1280,4480]{3,2,1,0:T(8,128)(2,1)} async-done(((bf16[1,2,40,4480]{3,2,1,0:T(8,128)(2,1)}), bf16[1,2,1280,4480]{3,2,1,0:T(8,128)(2,1)}) %all-gather.12.cloned.1.call-update) | async-done | bytes 22937616 | tf_op jit(solution)/reshape | solution.py:58
  1365.1 83.5 %all-gather.10.cloned.1.call-done = bf16[1,2,1280,4480]{3,2,1,0:T(8,128)(2,1)} async-done(((bf16[1,2,40,4480]{3,2,1,0:T(8,128)(2,1)}), bf16[1,2,1280,4480]{3,2,1,0:T(8,128)(2,1)}) %all-gather.10.cloned.1.call-update) | async-done | bytes 22937616 | tf_op jit(solution)/reshape | solution.py:58
  1448.6 15.8 %copy.30 = bf16[2,1280,4480]{2,1,0:T(8,128)(2,1)} copy(bf16[2,1280,4480]{2,1,0:T(8,128)(2,1)} %bitcast.356) | data formatting | bytes 45875200
  1464.5 6.7 copy-done
  1471.2 8.2 copy.31
  (67 shorter events, 6.4 us)
Async XLA Ops:
  7.2 992.5 %reduce-scatter.29.cloned.1.call-start = ((), (), s32[]{:S(2)}) async-start(), calls=%async_computation.10 | async-start | bytes 23654400
  10.8 40.0 %slice-start = ((s8[5242880]{0:T(1024)(128)(4,1)}), s8[1048576]{0:T(1024)(128)(4,1)S(1)}, s32[]{:S(2)}) async-start(s8[5242880]{0:T(1024)(128)(4,1)} %bitcast.357), calls=%async_computation.11 | async-start | bytes 2097152
  18.8 32.0 %copy-start.13 = (f32[2048]{0:T(1024)}, f32[2048]{0:T(1024)S(1)}, u32[]{:S(2)}) copy-start(f32[2048]{0:T(1024)S(1)} %add_rsqrt_fusion) | copy-start | bytes 24580
  18.8 32.0 %slice-start.1 = ((s8[5242880]{0:T(1024)(128)(4,1)}), s8[4194304]{0:T(1024)(128)(4,1)S(1)}, s32[]{:S(2)}) async-start(s8[5242880]{0:T(1024)(128)(4,1)} %bitcast.357), calls=%async_computation.12 | async-start | bytes 8388608
  144.7 0.6 copy-start.8
  144.7 32.8 %copy-start.10 = (f32[1,2048]{1,0:T(1,128)}, f32[1,2048]{1,0:T(1,128)S(1)}, u32[]{:S(2)}) copy-start(f32[1,2048]{1,0:T(1,128)S(1)} %rsqrt.32) | copy-start | bytes 24580
  145.3 32.3 %copy-start.1 = (bf16[1,2048,1280]{1,2,0:T(8,128)(2,1)S(1)}, bf16[1,2048,1280]{1,2,0:T(8,128)(2,1)}, u32[]{:S(2)}) copy-start(bf16[1,2048,1280]{1,2,0:T(8,128)(2,1)} %get-tuple-element.28) | copy-start | bytes 15728644
  145.3 62.9 %slice-start.2 = ((s8[5242880]{0:T(1024)(128)(4,1)}), s8[4194304]{0:T(1024)(128)(4,1)S(1)}, s32[]{:S(2)}) async-start(s8[5242880]{0:T(1024)(128)(4,1)} %bitcast.359), calls=%async_computation.13 | async-start | bytes 8388608
  177.5 30.7 %slice-start.3 = ((s8[5242880]{0:T(1024)(128)(4,1)}), s8[1048576]{0:T(1024)(128)(4,1)S(1)}, s32[]{:S(2)}) async-start(s8[5242880]{0:T(1024)(128)(4,1)} %bitcast.359), calls=%async_computation.14 | async-start | bytes 2097152
  314.7 36.9 %copy-start.9 = (f32[2048]{0:T(1024)S(1)}, f32[2048]{0:T(1024)}, u32[]{:S(2)}) copy-start(f32[2048]{0:T(1024)} %copy-done.8) | copy-start | bytes 24580
  314.7 37.0 %copy-start.11 = (f32[1,2048]{1,0:T(1,128)S(1)}, f32[1,2048]{1,0:T(1,128)}, u32[]{:S(2)}) copy-start(f32[1,2048]{1,0:T(1,128)} %copy-done.10) | copy-start | bytes 24580
  364.0 31.5 %copy-start.14 = (f32[2048]{0:T(1024)S(1)}, f32[2048]{0:T(1024)}, u32[]{:S(2)}) copy-start(f32[2048]{0:T(1024)} %copy-done.13) | copy-start | bytes 24580
  434.4 0.7 copy-start.12
  434.5 566.4 %reduce-scatter.27.cloned.1.call-start = ((), (), s32[]{:S(2)}) async-start(), calls=%async_computation.9 | async-start | bytes 23654400
  473.2 543.2 %reduce-scatter.25.cloned.1.call-start = ((), (), s32[]{:S(2)}) async-start(), calls=%async_computation.8 | async-start | bytes 23654400
  521.0 626.4 %reduce-scatter.23.cloned.1.call-start = ((), (), s32[]{:S(2)}) async-start(), calls=%async_computation.7 | async-start | bytes 23654400
  552.0 729.8 %all-gather.14.cloned.1.call-start = ((), (), s32[]{:S(2)}) async-start(), calls=%async_computation.6 | async-start | bytes 23654400 | tf_op jit(solution)/reshape | solution.py:58
  773.0 219.7 %collective-permute-start = (bf16[124,1280]{1,0:T(8,128)(2,1)S(1)}, bf16[124,1280]{1,0:T(8,128)(2,1)S(1)}, u32[]{:S(2)}, u32[]{:S(2)}) collective-permute-start(bf16[124,1280]{1,0:T(8,128)(2,1)S(1)} %slice.24), channel_id=1, source_target_pairs={{0,1},{1,2},{2,3},{3,4},{4,5},{5,6},{6,7},{7,8},{8,9},{9,10},{10,1... | collective-permute-start | bytes 952328
  988.3 8.4 collective-permute-start.1
  997.9 0.7 copy-start.2
  1000.8 2.3 copy-start.5
  1002.2 15.4 %copy-start.7 = (bf16[1,1,40,4480]{3,2,1,0:T(8,128)(2,1)}, bf16[1,1,40,4480]{3,2,1,0:T(8,128)(2,1)S(1)}, u32[]{:S(2)}) copy-start(bf16[1,1,40,4480]{3,2,1,0:T(8,128)(2,1)S(1)} %convert_bitcast_fusion.4) | copy-start | bytes 1075204
  1017.5 180.0 %copy-start.3 = (bf16[1,1,40,4480]{3,2,1,0:T(8,128)(2,1)}, bf16[1,1,40,4480]{3,2,1,0:T(8,128)(2,1)S(1)}, u32[]{:S(2)}) copy-start(bf16[1,1,40,4480]{3,2,1,0:T(8,128)(2,1)S(1)} %convert_bitcast_fusion.5) | copy-start | bytes 1075204
  1148.6 49.0 %copy-start.6 = (bf16[1,1,40,4480]{3,2,1,0:T(8,128)(2,1)}, bf16[1,1,40,4480]{3,2,1,0:T(8,128)(2,1)S(1)}, u32[]{:S(2)}) copy-start(bf16[1,1,40,4480]{3,2,1,0:T(8,128)(2,1)S(1)} %convert_bitcast_fusion.6) | copy-start | bytes 1075204
  1200.6 6.8 copy-start.4
  1202.1 163.0 %all-gather.12.cloned.1.call-start = ((), (), s32[]{:S(2)}) async-start(), calls=%async_computation.5 | async-start | bytes 23654400 | tf_op jit(solution)/reshape | solution.py:58
  1207.0 241.6 %all-gather.10.cloned.1.call-start = ((), (), s32[]{:S(2)}) async-start(), calls=%async_computation.4 | async-start | bytes 23654400 | tf_op jit(solution)/reshape | solution.py:58
  1448.6 22.5 %copy-start = (bf16[1,2,1280,4480]{3,2,1,0:T(8,128)(2,1)S(1)}, bf16[1,2,1280,4480]{3,2,1,0:T(8,128)(2,1)}, u32[]{:S(2)}) copy-start(bf16[1,2,1280,4480]{3,2,1,0:T(8,128)(2,1)} %all-gather.12.cloned.1.call-done) | copy-start | bytes 68812800
Sparse Core Ops, SparseCore 0:
  434.6 130.1 reduce-scatter.28
  568.7 231.3 reduce-scatter.26
  804.5 211.8 reduce-scatter.24
  1020.6 126.7 reduce-scatter.22
  1202.2 79.4 all-gather.13
  1284.3 80.6 all-gather.11
  1367.8 80.7 all-gather.9
where the time goes:
time: 1500 us; the launch traced here: 1490 us
  matrix products  517 us (34%)
  blocking collectives  405 us (27%)
  waiting for transfers between devices  356 us (24%)
  other arithmetic  103 us (7%)
  local copies, waits for them, and re-layouts  79.3 us (5%)
  between operations  17.6 us (1%)
    unnamed x2, blocking collectives  359 us
    reshape x3, waiting for transfers between devices, step(): t.reshape(-1, *t.shape[2:])  209 us
    dot_general x5, matrix products, layer(): gate = jnp.dot(a, w['w_gate'], preferred_element_type=jnp.float32)  175 us
    dot_general x5, matrix products, layer(): up = jnp.dot(a, w['w_up'], preferred_element_type=jnp.float32)  174 us
    dot_general x5, matrix products, matmul(): jnp.dot(a, w, preferred_element_type=jnp.float32).astype(jnp.bfloat16)  168 us
    unnamed x13, waiting for transfers between devices  146 us
    unnamed x5, other arithmetic  79.1 us
    unnamed x49, local copies, waits for them, and re-layouts  77.7 us
  transfers between devices with their start and end apart: 9, of which 6 were waited for; matrix products, arithmetic and copies ran while one was open for 40% of the time, Pallas kernels for 0%

commit v1 on v0

v1 whole, which is shorter than its diff:
```python
import math

import jax
import jax.numpy as jnp
from jax import lax
from jax.experimental import pallas as pl
from jax.experimental.pallas import tpu as pltpu
from jax.sharding import PartitionSpec as P

BF = jnp.bfloat16
F32 = jnp.float32
VMEM_LIMIT = 66_900_000
NN = (((1,), (0,)), ((), ()))
TN = (((0,), (0,)), ((), ()))
NT = (((1,), (1,)), ((), ()))
SIDE = 4
STEP = 640
TOK = 512


def dot(a, b, form):
    return lax.dot_general(a, b, form, preferred_element_type=F32)


def sigmoid(g):
    return 0.5 * jnp.tanh(0.5 * g) + 0.5


def whole(shape):
    return pl.BlockSpec(shape, lambda *_: (0,) * len(shape), pipeline_mode=pl.Buffered(1))


def params(**kw):
    return pltpu.CompilerParams(vmem_limit_bytes=VMEM_LIMIT, **kw)


def norm_rows(h):
    scale = lax.rsqrt(jnp.mean(h * h, 0, keepdims=True) + 1e-6)
    return h * scale


def first_kernel(x_ref, wg_ref, wu_ref, xT_ref, aT_ref, g_ref, u_ref, act_ref):
    tokens = x_ref.shape[0]

    @pl.when(pl.program_id(0) == 0)
    def _():
        def turn(i, _):
            at = pl.ds(pl.multiple_of(i * 128, 128), 128)
            part = x_ref[at, :].astype(F32).T
            xT_ref[:, at] = part.astype(BF)
            aT_ref[:, at] = norm_rows(part).astype(BF)
            return 0

        lax.fori_loop(0, tokens // 128, turn, 0)

    g = dot(wg_ref[...], aT_ref[...], TN)
    g_ref[...] = g
    u = dot(wu_ref[...], aT_ref[...], TN)
    u_ref[...] = u
    act_ref[...] = (g * sigmoid(g) * u).astype(BF)


def first(layer, x, w_gate, w_up):
    tokens, d = x.shape
    ff = w_gate.shape[-1]
    wspec = pl.BlockSpec((None, d, STEP), lambda j: (layer, 0, j))
    hidden = pl.BlockSpec((STEP, tokens), lambda j: (j, 0))
    return pl.pallas_call(
        first_kernel,
        name="first",
        grid=(ff // STEP,),
        in_specs=[whole((tokens, d)), wspec, wspec],
        out_specs=[whole((d, tokens)), whole((d, tokens)), hidden, hidden, hidden],
        out_shape=[
            jax.ShapeDtypeStruct((d, tokens), BF),
            jax.ShapeDtypeStruct((d, tokens), BF),
            jax.ShapeDtypeStruct((ff, tokens), F32),
            jax.ShapeDtypeStruct((ff, tokens), F32),
            jax.ShapeDtypeStruct((ff, tokens), BF),
        ],
        compiler_params=params(),
    )(x, w_gate, w_up)


def down_kernel(wd_ref, act_ref, xT_ref, hT_ref, aT_ref):
    out = dot(wd_ref[...], act_ref[...], TN).astype(BF)
    h = xT_ref[...] + out
    hT_ref[...] = h
    aT_ref[...] = norm_rows(h.astype(F32)).astype(BF)


def down(layer, w_down, act, xT):
    d, tokens = xT.shape
    ff = act.shape[0]
    column = pl.BlockSpec((d, TOK), lambda i: (0, i))
    return pl.pallas_call(
        down_kernel,
        name="down",
        grid=(tokens // TOK,),
        in_specs=[
            pl.BlockSpec((None, ff, d), lambda i: (layer, 0, 0), pipeline_mode=pl.Buffered(1)),
            pl.BlockSpec((ff, TOK), lambda i: (0, i)),
            column,
        ],
        out_specs=[column, column],
        out_shape=[jax.ShapeDtypeStruct((d, tokens), BF)] * 2,
        compiler_params=params(),
    )(w_down, act, xT)


def hidden_back(g, u, da):
    da = da.astype(F32)
    s = sigmoid(g)
    silu = g * s
    return (da * u * (s + silu * (1.0 - s))).astype(BF), (da * silu).astype(BF)


def last_kernel(dy_ref, aT_ref, wg_ref, wu_ref, wd_ref, dyT_ref, act_ref, dgu_ref):
    tokens = dy_ref.shape[0]

    @pl.when(pl.program_id(0) == 0)
    def _():
        def turn(i, _):
            at = pl.ds(pl.multiple_of(i * 128, 128), 128)
            dyT_ref[:, at] = dy_ref[at, :].astype(F32).T.astype(BF)
            return 0

        lax.fori_loop(0, tokens // 128, turn, 0)

    g = dot(wg_ref[...], aT_ref[...], TN)
    u = dot(wu_ref[...], aT_ref[...], TN)
    da = dot(wd_ref[...], dyT_ref[...], NN).astype(BF)
    act_ref[...] = (g * sigmoid(g) * u).astype(BF)
    dgu_ref[0], dgu_ref[1] = hidden_back(g, u, da)


def last(layer, dy, aT, w_gate, w_up, w_down):
    d, tokens = aT.shape
    ff = w_gate.shape[-1]
    wspec = pl.BlockSpec((None, d, STEP), lambda j: (layer, 0, j))
    return pl.pallas_call(
        last_kernel,
        name="last",
        grid=(ff // STEP,),
        in_specs=[whole((tokens, d)), whole((d, tokens)), wspec, wspec, pl.BlockSpec((None, STEP, d), lambda j: (layer, j, 0))],
        out_specs=[
            whole((d, tokens)),
            pl.BlockSpec((STEP, tokens), lambda j: (j, 0)),
            pl.BlockSpec((2, STEP, tokens), lambda j: (0, j, 0)),
        ],
        out_shape=[
            jax.ShapeDtypeStruct((d, tokens), BF),
            jax.ShapeDtypeStruct((ff, tokens), BF),
            jax.ShapeDtypeStruct((2, ff, tokens), BF),
        ],
        compiler_params=params(),
    )(dy, aT, w_gate, w_up, w_down)


def input_kernel(wg_ref, wu_ref, dg_ref, du_ref, hT_ref, dyT_ref, dhT_ref):
    da = dot(wg_ref[...], dg_ref[...], NN).astype(BF) + dot(wu_ref[...], du_ref[...], NN).astype(BF)
    h = hT_ref[...].astype(F32)
    da = da.astype(F32)
    scale = lax.rsqrt(jnp.mean(h * h, 0, keepdims=True) + 1e-6)
    along = jnp.mean(da * h, 0, keepdims=True)
    dh = da * scale - h * (scale * scale * scale * along)
    dhT_ref[...] = dyT_ref[...] + dh.astype(BF)


def back_input(layer, w_gate, w_up, dgu, hT, dyT):
    d, tokens = hT.shape
    ff = w_gate.shape[-1]
    wspec = pl.BlockSpec((None, d, ff), lambda i: (layer, 0, 0), pipeline_mode=pl.Buffered(1))
    column = pl.BlockSpec((d, TOK), lambda i: (0, i))
    return pl.pallas_call(
        input_kernel,
        name="back_input",
        grid=(tokens // TOK,),
        in_specs=[
            wspec,
            wspec,
            pl.BlockSpec((None, ff, TOK), lambda i: (0, 0, i)),
            pl.BlockSpec((None, ff, TOK), lambda i: (1, 0, i)),
            column,
            column,
        ],
        out_specs=column,
        out_shape=jax.ShapeDtypeStruct((d, tokens), BF),
        compiler_params=params(),
    )(w_gate, w_up, dgu, dgu, hT, dyT)


def hidden_kernel(wd_ref, dhT_ref, g_ref, u_ref, dgu_ref):
    da = dot(wd_ref[...], dhT_ref[...], NN).astype(BF)
    dgu_ref[0], dgu_ref[1] = hidden_back(g_ref[...], u_ref[...], da)


def back_hidden(layer, w_down, dhT, g, u):
    d, tokens = dhT.shape
    ff = g.shape[0]
    hidden = pl.BlockSpec((STEP, tokens), lambda j: (j, 0))
    return pl.pallas_call(
        hidden_kernel,
        name="back_hidden",
        grid=(ff // STEP,),
        in_specs=[pl.BlockSpec((None, STEP, d), lambda j: (layer, j, 0)), whole((d, tokens)), hidden, hidden],
        out_specs=pl.BlockSpec((2, STEP, tokens), lambda j: (0, j, 0)),
        out_shape=jax.ShapeDtypeStruct((2, ff, tokens), BF),
        compiler_params=params(),
    )(w_down, dhT, g, u)


OFF_A, OFF_B, OFF_C, OFF_D, OFF_F = 0, 1, 3, 4, 6
N_R0, N_SB, N_RB, N_SC, N_RC, N_SD, N_RD, N_SO = 5, 2, 5, 2, 3, 2, 4, 2
MESH = pl.DeviceIdType.MESH


class Place:
    def __init__(self):
        me = lax.axis_index("dp")
        self.core = me % 2
        self.y = (me // 2) % SIDE
        self.x = me // (2 * SIDE)

    def number(self, x, y, core):
        return ((x % SIDE) * SIDE + y % SIDE) * 2 + core

    def other_core(self):
        return self.number(self.x, self.y, 1 - self.core)

    def first(self, odd):
        return self.x + odd * (self.y - self.x), self.y + odd * (self.x - self.y)

    def along_first(self, odd, by):
        return self.number(self.x + (1 - odd) * by, self.y + odd * by, self.core)

    def along_second(self, odd, by):
        return self.number(self.x + odd * by, self.y + (1 - odd) * by, self.core)


class Reducer:
    def __init__(self, rows, width, slots):
        self.rows, self.width, self.slots = rows, width, slots

    def scratch(self):
        r, w = self.rows, self.width
        dma = pltpu.SemaphoreType.DMA
        return [
            pltpu.VMEM((self.slots, SIDE, SIDE, 2, r, w), BF),
            pltpu.VMEM((N_R0, SIDE, SIDE, r, w), BF),
            pltpu.VMEM((N_SB, 2, 4, r, w), BF),
            pltpu.VMEM((N_RB, 2, 4, r, w), BF),
            pltpu.VMEM((N_SC, 2, 2, r, w), BF),
            pltpu.VMEM((N_RC, 2, 2, r, w), BF),
            pltpu.VMEM((N_SD, 3, r, w), BF),
            pltpu.VMEM((N_RD, 3, r, w), BF),
            pltpu.VMEM((N_SO, r, w), F32),
            dma((self.slots,)),
            dma((N_R0,)),
            dma((N_R0,)),
            dma((N_SB, 2)),
            dma((N_RB, 2)),
            dma((N_SC, 2)),
            dma((N_RC, 2)),
            dma((N_SD, 3)),
            dma((N_RD, 3)),
        ]

    def bind(self, place, refs, finish, load=None):
        self.place, self.finish, self.load = place, finish, load
        (self.G, self.R0, self.SB, self.RB, self.SC, self.RC, self.SD, self.RD, self.SO) = refs[:9]
        (self.l_sem, self.a_send, self.a_recv, self.b_send, self.b_recv, self.c_send, self.c_recv, self.d_send, self.d_recv) = refs[9:]

    def remote(self, src, dst, send, recv, to):
        return pltpu.make_async_remote_copy(src_ref=src, dst_ref=dst, send_sem=send, recv_sem=recv, device_id={"dp": to}, device_id_type=MESH)

    def copy_a(self, k):
        core = self.place.core
        s = k % N_R0
        return self.remote(self.G.at[k % self.slots, :, :, 1 - core], self.R0.at[s], self.a_send.at[s], self.a_recv.at[s], self.place.other_core())

    def copy_b(self, k, way):
        s, r = k % N_SB, k % N_RB
        to = self.place.along_first(k % 2, 1 if way == 0 else SIDE - 1)
        return self.remote(self.SB.at[s, way], self.RB.at[r, way], self.b_send.at[s, way], self.b_recv.at[r, way], to)

    def copy_c(self, k, way):
        s, r = k % N_SC, k % N_RC
        to = self.place.along_first(k % 2, 1 if way == 0 else SIDE - 1)
        return self.remote(self.SC.at[s, way], self.RC.at[r, way], self.c_send.at[s, way], self.c_recv.at[r, way], to)

    def copy_d(self, k, by):
        s, r = k % N_SD, k % N_RD
        to = self.place.along_second(k % 2, by)
        return self.remote(self.SD.at[s, by - 1], self.RD.at[r, by - 1], self.d_send.at[s, by - 1], self.d_recv.at[r, by - 1], to)

    def pair(self, k, target, j):
        odd = k % 2
        x = target + odd * (j - target)
        y = j + odd * (target - j)
        return self.G[k % self.slots, x, y, self.place.core].astype(F32) + self.R0[k % N_R0, x, y].astype(F32)

    def stage_a(self, k):
        if self.load is not None:
            self.load(k, k % self.slots).wait()
        self.copy_a(k).start()

    def stage_b(self, k):
        a = self.copy_a(k)
        a.wait_recv()
        a.wait_send()
        first, _ = self.place.first(k % 2)
        s = k % N_SB
        for way in range(2):
            for j in range(4):
                far = (j < 2) == (way == 0)
                target = (first + (2 if far else 1 if way == 0 else SIDE - 1)) % SIDE
                self.SB[s, way, j] = self.pair(k, target, j).astype(BF)
            self.copy_b(k, way).start()

    def stage_c(self, k):
        first, _ = self.place.first(k % 2)
        s, r = k % N_SC, k % N_RB
        for way in range(2):
            b = self.copy_b(k, way)
            b.wait_send()
            b.wait_recv()
            target = (first + (1 if way == 0 else SIDE - 1)) % SIDE
            for i in range(2):
                j = i + 2 * way
                self.SC[s, way, i] = (self.pair(k, target, j) + self.RB[r, way, j].astype(F32)).astype(BF)
            self.copy_c(k, way).start()

    def stage_d(self, k):
        for way in range(2):
            c = self.copy_c(k, way)
            c.wait_send()
            c.wait_recv()
        first, second = self.place.first(k % 2)
        b, c = k % N_RB, k % N_RC
        for by in (1, 2, 3, 0):
            j = (second + by) % SIDE
            high = j // 2
            total = self.pair(k, first, j) + self.RC[c, high, j % 2].astype(F32) + self.RB[b, 1 - high, j].astype(F32)
            if by:
                self.SD[k % N_SD, by - 1] = total.astype(BF)
                self.copy_d(k, by).start()
            else:
                self.SO[k % N_SO] = total

    def stage_f(self, k):
        total = self.SO[k % N_SO]
        for by in (1, 2, 3):
            d = self.copy_d(k, by)
            d.wait_send()
            d.wait_recv()
            total = total + self.RD[k % N_RD, by - 1].astype(F32)
        self.finish(k, total.astype(BF))

    def tick(self, t, low, high):
        for off, stage in ((OFF_F, self.stage_f), (OFF_D, self.stage_d), (OFF_C, self.stage_c), (OFF_B, self.stage_b), (OFF_A, self.stage_a)):
            k = t - off

            @pl.when(jnp.logical_and(k >= low, k < high))
            def _():
                stage(k)

        if self.load is not None:
            k = t + 1

            @pl.when(jnp.logical_and(k >= low, k < high))
            def _():
                self.load(k, k % self.slots).start()


def weights_kernel(shape, *refs):
    layers, d, ff, tokens, own_gu, own_dn, pad_dn = shape
    ins = refs[: 4 * layers]
    refs = refs[4 * layers :]
    gu_out, dn_out, ssq_out, gdn = refs[:4]
    res, stream, stage, ssq, peer = refs[4:9]
    res_sem, stream_sem, stage_sem, q_send, q_recv = refs[9:14]
    eng = refs[14:]
    place = Place()
    width_gu, width_dn = STEP, 128
    gu_chunks, dn_chunks = 2 * ff // width_gu, d // width_dn
    gu = Reducer(own_gu, width_gu, 7)
    dn = Reducer(pad_dn, width_dn, 5)

    barrier = pltpu.get_barrier_semaphore()
    others = [place.other_core()] + [f(0, by) for by in (1, 2, 3) for f in (place.along_first, place.along_second)]
    for other in others:
        pl.semaphore_signal(barrier, inc=1, device_id={"dp": other}, device_id_type=MESH)
    pl.semaphore_wait(barrier, len(others))

    ssq[...] = jnp.zeros_like(ssq)
    stage[:, :, pad_dn - 8 :, :] = jnp.zeros((2, 4, 8, d), BF)

    def add_squares(g, rows):
        g = g.astype(F32)
        if rows != g.shape[0]:
            g = jnp.where(lax.broadcasted_iota(jnp.int32, g.shape, 0) < rows, g, 0.0)
        g = g * g
        total = g[0:8]
        for i in range(8, g.shape[0], 8):
            total = total + g[i : i + 8]
        lanes = total[:, 0:128]
        for i in range(128, g.shape[1], 128):
            lanes = lanes + total[:, i : i + 128]
        ssq[0] = ssq[0] + lanes

    def finish_gu(k, g):
        gu_out[layers - 1 - k // gu_chunks, :, pl.ds(pl.multiple_of((k % gu_chunks) * width_gu, 128), width_gu)] = g
        add_squares(g, own_gu)

    def finish_dn(k, g):
        dn_out[layers - 1 - k // dn_chunks, :, pl.ds(pl.multiple_of((k % dn_chunks) * width_dn, 128), width_dn)] = g
        add_squares(g, own_dn)

    def load_dn(k, slot):
        at = pl.ds(pl.multiple_of((k % dn_chunks) * width_dn, 128), width_dn)
        return pltpu.make_async_copy(gdn.at[k // dn_chunks, :, :, :, :, at], dn.G.at[slot], dn.l_sem.at[slot])

    n = len(gu.scratch())
    gu.bind(place, eng[:n], finish_gu)
    dn.bind(place, eng[n:], finish_dn, load_dn)

    gu_tile = 2 * STEP
    gu_tiles = 2 * ff // gu_tile
    dn_tile = 4 * own_dn
    dn_tiles = ff // dn_tile

    def stream_gu(layer):
        def copy(i, slot):
            rows = pl.ds(pl.multiple_of(i * gu_tile, 128), gu_tile)
            return pltpu.make_async_copy(ins[4 * layer + 1].at[rows, :], stream.at[slot], stream_sem.at[slot])

        return copy

    def stream_dn(layer):
        def copy(i, slot):
            rows = pl.ds(pl.multiple_of(i * dn_tile, 16), dn_tile)
            return pltpu.make_async_copy(ins[4 * layer + 3].at[rows, :], stream.at[slot, pl.ds(0, dn_tile)], stream_sem.at[slot])

        return copy

    def resident(ref):
        return pltpu.make_async_copy(ref, res, res_sem)

    def compute_gu(first_chunk):
        def run(i, slot, half):
            acc = dot(res[half * (d // 2) : (half + 1) * (d // 2), :], stream[slot], NT)
            for h in range(2):
                at = (first_chunk + 2 * i + h) % gu.slots
                for q in range(SIDE * SIDE):
                    x, y, core = half * 2 + q // (2 * SIDE), (q // 2) % SIDE, q % 2
                    gu.G[at, x, y, core] = acc[q * own_gu : (q + 1) * own_gu, h * STEP : (h + 1) * STEP].astype(BF)

        return run

    def out_dn(layer, i, slot):
        return pltpu.make_async_copy(
            stage.at[slot], gdn.at[layers - 1 - layer, i // 2, pl.ds((i % 2) * 2, 2)].reshape(4, pad_dn, d), stage_sem.at[slot]
        )

    def compute_dn(layer):
        def run(i, slot):
            s = i % 2

            @pl.when(i >= 2)
            def _():
                out_dn(layer, i - 2, s).wait()

            acc = dot(stream[slot, 0:dn_tile, :], res[...], NT)
            for q in range(4):
                stage[s, q, 0:own_dn, :] = acc[q * own_dn : (q + 1) * own_dn].astype(BF)
            out_dn(layer, i, s).start()

        return run

    top = layers - 1
    phases = []
    phases.append(("gu", top, ins[4 * top + 0], gu_tiles, stream_gu(top)))
    for layer in range(top, -1, -1):
        phases.append(("dn", layer, ins[4 * layer + 2], dn_tiles, stream_dn(layer)))
    for layer in range(top - 1, -1, -1):
        phases.append(("gu", layer, ins[4 * layer + 0], gu_tiles, stream_gu(layer)))

    resident(phases[0][2]).start()
    phases[0][4](0, 0).start()
    base = 0
    gu_t, gu_high = 0, 0
    dn_t, dn_low = 0, 0
    lag = OFF_F + 1
    for number, (kind, layer, ref, tiles, copy) in enumerate(phases):
        following = phases[number + 1] if number + 1 < len(phases) else None
        resident(ref).wait()
        gu_first = gu_high
        if kind == "gu":
            gu_high += gu_chunks
            gu_shift = gu_first - 2
        dn_on = number >= 2
        tick_low = 0
        gu_high_now = gu_high
        dn_high = dn_chunks * (min(number - 1, layers)) if dn_on else 0

        def body(i, _, kind=kind, layer=layer, tiles=tiles, copy=copy, base=base, following=following, gu_first=gu_first, dn_t=dn_t, number=number):
            slot = (base + i) % 2
            copy(i, slot).wait()

            @pl.when(i + 1 < tiles)
            def _():
                copy(i + 1, 1 - slot).start()

            if following is not None:

                @pl.when(i + 1 == tiles)
                def _():
                    following[4](0, 1 - slot).start()

            if kind == "gu":
                run = compute_gu(gu_first)
                for half in range(2):
                    if number >= 2:
                        dn.tick(dn_t + 2 * i + half, 0, layers * dn_chunks)
                    gu.tick(gu_first + 2 * i + half - 2, gu_first, gu_first + gu_chunks)
                    run(i, slot, half)
            else:
                if number == 1:
                    gu.tick(gu_chunks - 2 + i, 0, gu_chunks)
                else:
                    dn.tick(dn_t + i, 0, layers * dn_chunks)
                compute_dn(layer)(i, slot)
            return 0

        if number == 2:
            load_dn(0, 0).start()

        lax.fori_loop(0, tiles, body, 0)
        if kind == "dn":
            out_dn(layer, tiles - 2, tiles % 2).wait()
            out_dn(layer, tiles - 1, 1 - tiles % 2).wait()
        if following is not None:
            resident(following[2]).start()
        base += tiles
        if number >= 2:
            dn_t += 2 * tiles if kind == "gu" else tiles

    def drain(i, _):
        dn.tick(dn_t + i, 0, layers * dn_chunks)
        gu.tick(gu_high - 2 + i, gu_high - gu_chunks, gu_high)
        return 0

    lax.fori_loop(0, OFF_F + 2, drain, 0)

    for number, peers in enumerate(([place.other_core()], [place.along_first(0, by) for by in (1, 2, 3)], [place.along_second(0, by) for by in (1, 2, 3)])):
        at = (0, 1, 4)[number]
        copies = []
        for i, to in enumerate(peers):
            copies.append(
                pltpu.make_async_remote_copy(
                    src_ref=ssq.at[number], dst_ref=peer.at[at + i], send_sem=q_send.at[at + i], recv_sem=q_recv.at[at + i], device_id={"dp": to}, device_id_type=MESH
                )
            )
            copies[-1].start()
        total = ssq[number]
        for i, one in enumerate(copies):
            one.wait_recv()
            total = total + peer[at + i]
        for one in copies:
            one.wait_send()
        if number < 2:
            ssq[number + 1] = total
        else:
            ssq_out[...] = total


def weight_gradients(parts, n):
    layers = len(parts)
    d, tokens = parts[0][0].shape
    ff = parts[0][3].shape[0]
    own_gu, own_dn = d // n, ff // n
    pad_dn = -(-own_dn // 8) * 8
    shape = (layers, d, ff, tokens, own_gu, own_dn, pad_dn)
    dma = pltpu.SemaphoreType.DMA
    flat = []
    for aT, dgu, dhT, act in parts:
        flat += [aT, dgu.reshape(2 * ff, tokens), dhT, act]
    vm = pl.BlockSpec(memory_space=pltpu.VMEM)
    hbm = pl.BlockSpec(memory_space=pl.ANY)
    flops = 2 * 3 * layers * d * ff * tokens
    out = pl.pallas_call(
        lambda *refs: weights_kernel(shape, *refs),
        name="weights",
        in_specs=[hbm] * len(flat),
        out_specs=[vm, vm, vm, hbm],
        out_shape=[
            jax.ShapeDtypeStruct((layers, own_gu, 2 * ff), BF),
            jax.ShapeDtypeStruct((layers, pad_dn, d), BF),
            jax.ShapeDtypeStruct((8, 128), F32),
            jax.ShapeDtypeStruct((layers, SIDE, SIDE, 2, pad_dn, d), BF),
        ],
        scratch_shapes=[
            pltpu.VMEM((d, tokens), BF),
            pltpu.VMEM((2, 2 * STEP, tokens), BF),
            pltpu.VMEM((2, 4, pad_dn, d), BF),
            pltpu.VMEM((3, 8, 128), F32),
            pltpu.VMEM((7, 8, 128), F32),
            dma,
            dma((2,)),
            dma((2,)),
            dma((7,)),
            dma((7,)),
        ]
        + Reducer(own_gu, STEP, 7).scratch()
        + Reducer(pad_dn, 128, 5).scratch(),
        compiler_params=params(collective_id=1, has_side_effects=True),
        cost_estimate=pl.CostEstimate(flops=flops, bytes_accessed=2**27, transcendentals=0),
    )(*flat)
    return out[0], out[1][:, :own_dn], jnp.sum(out[2])


def adamw(w, m, v, g):
    m = 0.9 * m + 0.1 * g
    v = 0.95 * v + 0.05 * g * g
    step = m * lax.rsqrt(v + 1e-8) + 0.1 * w
    return (w - 0.02 * step).astype(BF), m, v


def solution(mesh):
    n = mesh.shape["dp"]
    assert n == 2 * SIDE * SIDE and math.isqrt(n // 2) == SIDE

    def one(x, dy, wg, wu, wd, *moments):
        x, dy = x[0], dy[0]
        ff = wg.shape[-1]
        xT, aT0, g0, u0, act0 = first(0, x, wg, wu)
        hT, aT1 = down(0, wd, act0, xT)
        dyT, act1, dgu1 = last(1, dy, aT1, wg, wu, wd)
        dhT = back_input(1, wg, wu, dgu1, hT, dyT)
        dgu0 = back_hidden(0, wd, dhT, g0, u0)
        gu, dn, squares = weight_gradients([(aT0, dgu0, dhT, act0), (aT1, dgu1, dyT, act1)], n)
        count = wg.size + wu.size + wd.size
        factor = jnp.minimum(1.0, 0.5 * lax.rsqrt(squares / count + 1e-30))
        gradients = (gu[:, :, :ff], gu[:, :, ff:], dn)
        me = lax.axis_index("dp")
        ws, ms, vs = [], [], []
        for w, m, v, g in zip((wg, wu, wd), moments[:3], moments[3:], gradients, strict=True):
            mine = lax.dynamic_slice_in_dim(w, me * m.shape[1], m.shape[1], 1)
            w, m, v = adamw(mine.astype(F32), m, v, g.astype(F32) * factor)
            ws.append(lax.all_gather(w, "dp", axis=1, tiled=True))
            ms.append(m)
            vs.append(v)
        return tuple(ws + ms + vs)

    seq = P(("rep", "dp"))
    own = P(None, "dp")
    return jax.shard_map(
        one,
        mesh=mesh,
        in_specs=(seq, seq, P(), P(), P()) + (own,) * 6,
        out_specs=(P("rep"),) * 3 + (P("rep", "dp"),) * 6,
        check_vma=False,
    )
```

time: 1500 us -> 918 us (0.61)
  Pallas kernels: 0 us -> 610 us
  matrix products: 517 us -> 0 us
  blocking collectives: 405 us -> 0 us
  waiting for transfers between devices: 356 us -> 215 us
  other arithmetic: 103 us -> 11.6 us
  local copies, waits for them, and re-layouts: 79.3 us -> 59.2 us
    pallas_call x0 -> x6, Pallas kernels: none -> 610 us  [the longest x1 301 us: weight_gradients(): pl.pallas_call(lambda *refs: weights_kernel(shape, *refs), name='weights'...]
    dot_general x15 -> x0, matrix products: 517 us -> none  [the longest x5 175 us: layer(): gate = jnp.dot(a, w['w_gate'], preferred_element_type=jnp.float32)]
    unnamed x2 -> x0, blocking collectives: 359 us -> none
    all_gather x0 -> x3, waiting for transfers between devices: none -> 214 us  [one(): ws.append(lax.all_gather(w, 'dp', axis=1, tiled=True))]
    reshape x3 -> x0, waiting for transfers between devices: 209 us -> none  [step(): t.reshape(-1, *t.shape[2:])]
    unnamed x13 -> x3, waiting for transfers between devices: 146 us -> 0.82 us
    unnamed x5 -> x0, other arithmetic: 79.1 us -> none
    reduce_sum x1 -> x0, blocking collectives: 45.3 us -> none  [of_a_group(): jnp.sum(g * g)]
  transfers between devices with their start and end apart: 9 -> 3, of which waited for: 6 -> 3; matrix products, arithmetic and copies ran while one was open for 40% -> 4% of each run, Pallas kernels for 0% -> 0%
where the time goes in v1:
time: 918 us; the launch traced here: 910 us
  Pallas kernels  610 us (66%)
  waiting for transfers between devices  215 us (23%)
  local copies, waits for them, and re-layouts  59.2 us (6%)
  between operations  14.9 us (2%)
  other arithmetic  11.6 us (1%)
    pallas_call x1, Pallas kernels, weight_gradients(): pl.pallas_call(lambda *refs: weights_kernel(shape, *refs), name='weights'...  301 us
    all_gather x3, waiting for transfers between devices, one(): ws.append(lax.all_gather(w, 'dp', axis=1, tiled=True))  214 us
    pallas_call x1, Pallas kernels, last(): pl.pallas_call(last_kernel, name='last', grid=(ff // STEP,), in_specs=[wh...  91 us
    pallas_call x1, Pallas kernels, back_input(): pl.pallas_call(input_kernel, name='back_input', grid=(tokens // TOK,), in...  68.1 us
    pallas_call x1, Pallas kernels, first(): pl.pallas_call(first_kernel, name='first', grid=(ff // STEP,), in_specs=[...  63.1 us
    unnamed x7, local copies, waits for them, and re-layouts  57.8 us
    pallas_call x1, Pallas kernels, back_hidden(): pl.pallas_call(hidden_kernel, name='back_hidden', grid=(ff // STEP,), in_...  51.8 us
    pallas_call x1, Pallas kernels, down(): pl.pallas_call(down_kernel, name='down', grid=(tokens // TOK,), in_specs=...  34.2 us
  transfers between devices with their start and end apart: 3, of which 3 were waited for; matrix products, arithmetic and copies ran while one was open for 4% of the time, Pallas kernels for 0%

profile of v1, /device:TPU:97, one launch (start us, length us, event | category | flops | bytes accessed | tf_op | source)
XLA Modules:
  0.0 910.2 jit_solution(18185821625817884805)
XLA Ops:
  7.2 0.1 all-gather.8.cloned.1.call-start
  7.3 63.1 %first.1 = (bf16[1280,2048]{1,0:T(8,128)(2,1)}, bf16[1280,2048]{1,0:T(8,128)(2,1)}, f32[4480,2048]{1,0:T(8,128)}, f32[4480,2048]{1,0:T(8,128)}, bf16[4480,2048]{1,0:T(8,128)(2,1)}) custom-call(bf16[2048,1280]{1,0:T(8,128)(2,1)} %bitcast.7, bf16[2,1280,4480]{2,1,0:T(8,128)(2,1)} %wg_ref.5, bf16[2,1280,4480]{2,1,0:T(8,128)(2,1)} %wu_ref.5), custom_call_target="tpu_custom_call" | custom-call | tf_op jit(solution)/shard_map/first/pallas_call | solution.py:68
  70.3 34.2 %down.1 = (bf16[1280,2048]{1,0:T(8,128)(2,1)}, bf16[1280,2048]{1,0:T(8,128)(2,1)}) custom-call(bf16[2,4480,1280]{2,1,0:T(8,128)(2,1)} %wd_ref.5, bf16[4480,2048]{1,0:T(8,128)(2,1)} %get-tuple-element.23.act_ref.refs_3_, bf16[1280,2048]{1,0:T(8,128)(2,1)} %get-tuple-element.24.xT_ref), custom_call_target="tpu_custom_call" | custom-call | tf_op jit(solution)/shard_map/down/pallas_call | solution.py:96
  104.5 91.0 %last.1 = (bf16[1280,2048]{1,0:T(8,128)(2,1)}, bf16[4480,2048]{1,0:T(8,128)(2,1)}, bf16[2,4480,2048]{2,1,0:T(8,128)(2,1)}) custom-call(bf16[2048,1280]{1,0:T(8,128)(2,1)} %bitcast.6, bf16[1280,2048]{1,0:T(8,128)(2,1)} %get-tuple-element.25.aT_ref.refs_4_, bf16[2,1280,4480]{2,1,0:T(8,128)(2,1)} %wg_ref.5, bf16[2,1280,4480]{2,1,0:T(8,128)(2,1)} %wu_ref.5, ...), custom_call_target="tpu_custom_call" | custom-call | tf_op jit(solution)/shard_map/last/pallas_call | solution.py:141
  195.5 68.1 %back_input.1.dhT_ref.refs_2_ = bf16[1280,2048]{1,0:T(8,128)(2,1)} custom-call(bf16[2,1280,4480]{2,1,0:T(8,128)(2,1)} %wg_ref.5, bf16[2,1280,4480]{2,1,0:T(8,128)(2,1)} %wu_ref.5, bf16[2,4480,2048]{2,1,0:T(8,128)(2,1)} %get-tuple-element.26.dg_ref.du_ref, bf16[2,4480,2048]{2,1,0:T(8,128)(2,1)} %get-tuple-element.26.dg_ref.du_ref, ...), custom_call_target="tpu_custom_call" | custom-call | tf_op jit(solution)/shard_map/back_input/pallas_call | solution.py:175
  263.7 51.8 %back_hidden.1 = bf16[2,4480,2048]{2,1,0:T(8,128)(2,1)} custom-call(bf16[2,4480,1280]{2,1,0:T(8,128)(2,1)} %wd_ref.5, bf16[1280,2048]{1,0:T(8,128)(2,1)} %back_input.1.dhT_ref.refs_2_, f32[4480,2048]{1,0:T(8,128)} %get-tuple-element.29.g_ref, f32[4480,2048]{1,0:T(8,128)} %get-tuple-element.30.u_ref), custom_call_target="tpu_custom_call" | custom-call | tf_op jit(solution)/shard_map/back_hidden/pallas_call | solution.py:202
  315.5 301.3 %weights.1 = (bf16[2,40,8960]{2,1,0:T(8,128)(2,1)}, bf16[2,144,1280]{2,1,0:T(8,128)(2,1)}, f32[8,128]{1,0:T(8,128)}, bf16[2,4,4,2,144,1280]{5,4,3,2,1,0:T(8,128)(2,1)}) custom-call(bf16[1280,2048]{1,0:T(8,128)(2,1)} %get-tuple-element.22.refs_0_, bf16[8960,2048]{1,0:T(8,128)(2,1)} %bitcast.5, bf16[1280,2048]{1,0:T(8,128)(2,1)} %back_input.1.dhT_ref.refs_2_, ...), custom_call_target="tpu_custom_call" | custom-call | flops 140928614400 | bytes 134217728 | tf_op jit(solution)/shard_map/weights/pallas_call | solution.py:592
  616.8 1.3 reduce_sum.9
  618.8 3.2 fusion.2
  622.0 1.4 copy.26
  623.4 0.1 all-gather.8.cloned.1.call-update
  623.5 0.1 all-gather.4.cloned.1.call-start
  623.5 7.1 fusion.10
  630.7 0.1 all-gather.4.cloned.1.call-update
  630.8 0.1 all-gather.6.cloned.1.call-start
  630.8 0.7 all-gather.6.cloned.1.call-update
  631.6 2.2 copy.28
  633.8 2.2 copy.29
  636.0 69.4 %all-gather.8.cloned.1.call-done = bf16[2,4480,1280]{2,0,1:T(2,128)(2,1)} async-done(((bf16[2,140,1280]{2,0,1:T(2,128)(2,1)}), bf16[2,4480,1280]{2,0,1:T(2,128)(2,1)}) %all-gather.8.cloned.1.call-update) | async-done | bytes 22937616 | tf_op jit(solution)/shard_map/all_gather | solution.py:651
  705.4 22.7 %copy.27 = bf16[2,4480,1280]{2,1,0:T(8,128)(2,1)} copy(bf16[2,4480,1280]{2,0,1:T(2,128)(2,1)} %all-gather.8.cloned.1.call-done) | data formatting | bytes 45875200
  728.1 60.9 %all-gather.4.cloned.1.call-done = bf16[2,1280,4480]{2,1,0:T(8,128)(2,1)} async-done(((bf16[2,40,4480]{2,1,0:T(8,128)(2,1)}), bf16[2,1280,4480]{2,1,0:T(8,128)(2,1)}) %all-gather.4.cloned.1.call-update) | async-done | bytes 22937616 | tf_op jit(solution)/shard_map/all_gather | solution.py:651
  788.9 83.5 %all-gather.6.cloned.1.call-done = bf16[2,1280,4480]{2,1,0:T(8,128)(2,1)} async-done(((bf16[2,40,4480]{2,1,0:T(8,128)(2,1)}), bf16[2,1280,4480]{2,1,0:T(8,128)(2,1)}) %all-gather.6.cloned.1.call-update) | async-done | bytes 22937616 | tf_op jit(solution)/shard_map/all_gather | solution.py:651
  872.5 0.0 copy-start
  872.5 15.8 %copy.40 = bf16[2,1280,4480]{2,1,0:T(8,128)(2,1)} copy(bf16[2,1280,4480]{2,1,0:T(8,128)(2,1)} %all-gather.4.cloned.1.call-done) | data formatting | bytes 45875200
  888.3 6.7 copy-done
  895.0 8.2 copy.41
Async XLA Ops:
  7.2 698.2 %all-gather.8.cloned.1.call-start = ((), (), s32[]{:S(2)}) async-start(), calls=%async_computation.2 | async-start | bytes 23654400 | tf_op jit(solution)/shard_map/all_gather | solution.py:651
  623.5 165.4 %all-gather.4.cloned.1.call-start = ((), (), s32[]{:S(2)}) async-start(), calls=%async_computation | async-start | bytes 23654400 | tf_op jit(solution)/shard_map/all_gather | solution.py:651
  630.8 241.7 %all-gather.6.cloned.1.call-start = ((), (), s32[]{:S(2)}) async-start(), calls=%async_computation.1 | async-start | bytes 23654400 | tf_op jit(solution)/shard_map/all_gather | solution.py:651
  872.5 22.5 %copy-start = (bf16[2,1280,4480]{2,1,0:T(8,128)(2,1)S(1)}, bf16[2,1280,4480]{2,1,0:T(8,128)(2,1)}, u32[]{:S(2)}) copy-start(bf16[2,1280,4480]{2,1,0:T(8,128)(2,1)} %all-gather.6.cloned.1.call-done) | copy-start | bytes 68812800
Sparse Core Ops, SparseCore 0:
  623.6 81.7 all-gather.7
  708.1 80.7 all-gather.3
  791.7 80.7 all-gather.5

commit v2 on v1

v2 whole, which is shorter than its diff:
```python
import math

import jax
import jax.numpy as jnp
from jax import lax
from jax.experimental import pallas as pl
from jax.experimental.pallas import tpu as pltpu
from jax.sharding import PartitionSpec as P

BF = jnp.bfloat16
F32 = jnp.float32
VMEM_LIMIT = 67_043_328
NN = (((1,), (0,)), ((), ()))
TN = (((0,), (0,)), ((), ()))
NT = (((1,), (1,)), ((), ()))
SIDE = 4
STEP = 640
TOK = 512


def dot(a, b, form):
    return lax.dot_general(a, b, form, preferred_element_type=F32)


def sigmoid(g):
    return 0.5 * jnp.tanh(0.5 * g) + 0.5


def whole(shape):
    return pl.BlockSpec(shape, lambda *_: (0,) * len(shape), pipeline_mode=pl.Buffered(1))


def params(**kw):
    return pltpu.CompilerParams(vmem_limit_bytes=VMEM_LIMIT, **kw)


def norm_rows(h):
    scale = lax.rsqrt(jnp.mean(h * h, 0, keepdims=True) + 1e-6)
    return h * scale


def first_kernel(x_ref, wg_ref, wu_ref, xT_ref, aT_ref, g_ref, u_ref, act_ref):
    tokens = x_ref.shape[0]

    @pl.when(pl.program_id(0) == 0)
    def _():
        def turn(i, _):
            at = pl.ds(pl.multiple_of(i * 128, 128), 128)
            part = x_ref[at, :].astype(F32).T
            xT_ref[:, at] = part.astype(BF)
            aT_ref[:, at] = norm_rows(part).astype(BF)
            return 0

        lax.fori_loop(0, tokens // 128, turn, 0)

    g = dot(wg_ref[...], aT_ref[...], TN)
    g_ref[...] = g
    u = dot(wu_ref[...], aT_ref[...], TN)
    u_ref[...] = u
    act_ref[...] = (g * sigmoid(g) * u).astype(BF)


def first(layer, x, w_gate, w_up):
    tokens, d = x.shape
    ff = w_gate.shape[-1]
    wspec = pl.BlockSpec((None, d, STEP), lambda j: (layer, 0, j))
    hidden = pl.BlockSpec((STEP, tokens), lambda j: (j, 0))
    return pl.pallas_call(
        first_kernel,
        name="first",
        grid=(ff // STEP,),
        in_specs=[whole((tokens, d)), wspec, wspec],
        out_specs=[whole((d, tokens)), whole((d, tokens)), hidden, hidden, hidden],
        out_shape=[
            jax.ShapeDtypeStruct((d, tokens), BF),
            jax.ShapeDtypeStruct((d, tokens), BF),
            jax.ShapeDtypeStruct((ff, tokens), F32),
            jax.ShapeDtypeStruct((ff, tokens), F32),
            jax.ShapeDtypeStruct((ff, tokens), BF),
        ],
        compiler_params=params(),
    )(x, w_gate, w_up)


def down_kernel(wd_ref, act_ref, xT_ref, hT_ref, aT_ref):
    out = dot(wd_ref[...], act_ref[...], TN).astype(BF)
    h = xT_ref[...] + out
    hT_ref[...] = h
    aT_ref[...] = norm_rows(h.astype(F32)).astype(BF)


def down(layer, w_down, act, xT):
    d, tokens = xT.shape
    ff = act.shape[0]
    column = pl.BlockSpec((d, TOK), lambda i: (0, i))
    return pl.pallas_call(
        down_kernel,
        name="down",
        grid=(tokens // TOK,),
        in_specs=[
            pl.BlockSpec((None, ff, d), lambda i: (layer, 0, 0), pipeline_mode=pl.Buffered(1)),
            pl.BlockSpec((ff, TOK), lambda i: (0, i)),
            column,
        ],
        out_specs=[column, column],
        out_shape=[jax.ShapeDtypeStruct((d, tokens), BF)] * 2,
        compiler_params=params(),
    )(w_down, act, xT)


def hidden_back(g, u, da):
    da = da.astype(F32)
    s = sigmoid(g)
    silu = g * s
    return (da * u * (s + silu * (1.0 - s))).astype(BF), (da * silu).astype(BF)


def last_kernel(dy_ref, aT_ref, wg_ref, wu_ref, wd_ref, dyT_ref, act_ref, dgu_ref):
    tokens = dy_ref.shape[0]

    @pl.when(pl.program_id(0) == 0)
    def _():
        def turn(i, _):
            at = pl.ds(pl.multiple_of(i * 128, 128), 128)
            dyT_ref[:, at] = dy_ref[at, :].astype(F32).T.astype(BF)
            return 0

        lax.fori_loop(0, tokens // 128, turn, 0)

    g = dot(wg_ref[...], aT_ref[...], TN)
    u = dot(wu_ref[...], aT_ref[...], TN)
    da = dot(wd_ref[...], dyT_ref[...], NN).astype(BF)
    act_ref[...] = (g * sigmoid(g) * u).astype(BF)
    dgu_ref[0], dgu_ref[1] = hidden_back(g, u, da)


def last(layer, dy, aT, w_gate, w_up, w_down):
    d, tokens = aT.shape
    ff = w_gate.shape[-1]
    wspec = pl.BlockSpec((None, d, STEP), lambda j: (layer, 0, j))
    return pl.pallas_call(
        last_kernel,
        name="last",
        grid=(ff // STEP,),
        in_specs=[whole((tokens, d)), whole((d, tokens)), wspec, wspec, pl.BlockSpec((None, STEP, d), lambda j: (layer, j, 0))],
        out_specs=[
            whole((d, tokens)),
            pl.BlockSpec((STEP, tokens), lambda j: (j, 0)),
            pl.BlockSpec((None, 2, STEP, tokens), lambda j: (j, 0, 0, 0)),
        ],
        out_shape=[
            jax.ShapeDtypeStruct((d, tokens), BF),
            jax.ShapeDtypeStruct((ff, tokens), BF),
            jax.ShapeDtypeStruct((ff // STEP, 2, STEP, tokens), BF),
        ],
        compiler_params=params(),
    )(dy, aT, w_gate, w_up, w_down)


OFF_A, OFF_B, OFF_C, OFF_D, OFF_F = 0, 1, 3, 5, 7
N_G, N_R0, N_SB, N_RB, N_SC, N_RC, N_SD, N_RD, N_SO = 8, 6, 2, 6, 2, 4, 2, 4, 2
WIDE = STEP
MESH = pl.DeviceIdType.MESH


class Place:
    def __init__(self):
        me = lax.axis_index("dp")
        self.core = me % 2
        self.y = (me // 2) % SIDE
        self.x = me // (2 * SIDE)

    def number(self, x, y, core):
        return ((x % SIDE) * SIDE + y % SIDE) * 2 + core

    def other_core(self):
        return self.number(self.x, self.y, 1 - self.core)

    def first(self, odd):
        return self.x + odd * (self.y - self.x), self.y + odd * (self.x - self.y)

    def along_first(self, odd, by):
        return self.number(self.x + (1 - odd) * by, self.y + odd * by, self.core)

    def along_second(self, odd, by):
        return self.number(self.x + odd * by, self.y + (1 - odd) * by, self.core)

    def meet(self):
        barrier = pltpu.get_barrier_semaphore()
        others = [self.other_core()] + [f(0, by) for by in (1, 2, 3) for f in (self.along_first, self.along_second)]
        for other in others:
            pl.semaphore_signal(barrier, inc=1, device_id={"dp": other}, device_id_type=MESH)
        pl.semaphore_wait(barrier, len(others))


class Reducer:
    @staticmethod
    def scratch(r, w):
        dma = pltpu.SemaphoreType.DMA
        return [
            pltpu.VMEM((N_G, SIDE, SIDE, 2, r, w), BF),
            pltpu.VMEM((N_R0, SIDE, SIDE, r, w), BF),
            pltpu.VMEM((N_SB, 2, 4, r, w), BF),
            pltpu.VMEM((N_RB, 2, 4, r, w), BF),
            pltpu.VMEM((N_SC, 2, 2, r, w), BF),
            pltpu.VMEM((N_RC, 2, 2, r, w), BF),
            pltpu.VMEM((N_SD, 3, r, w), BF),
            pltpu.VMEM((N_RD, 3, r, w), BF),
            pltpu.VMEM((N_SO, r, w), F32),
            dma((N_G,)),
            dma((N_R0,)),
            dma((N_R0,)),
            dma((N_SB, 2)),
            dma((N_RB, 2)),
            dma((N_SC, 2)),
            dma((N_RC, 2)),
            dma((N_SD, 3)),
            dma((N_RD, 3)),
        ]

    def __init__(self, place, refs, finish):
        self.place, self.finish = place, finish
        (self.G, self.R0, self.SB, self.RB, self.SC, self.RC, self.SD, self.RD, self.SO) = refs[:9]
        (self.l_sem, self.a_send, self.a_recv, self.b_send, self.b_recv, self.c_send, self.c_recv, self.d_send, self.d_recv) = refs[9:]

    def remote(self, src, dst, send, recv, to):
        return pltpu.make_async_remote_copy(src_ref=src, dst_ref=dst, send_sem=send, recv_sem=recv, device_id={"dp": to}, device_id_type=MESH)

    def copy_a(self, k):
        s = k % N_R0
        return self.remote(self.G.at[k % N_G, :, :, 1 - self.place.core], self.R0.at[s], self.a_send.at[s], self.a_recv.at[s], self.place.other_core())

    def copy_b(self, k, way):
        s, r = k % N_SB, k % N_RB
        to = self.place.along_first(k % 2, 1 if way == 0 else SIDE - 1)
        return self.remote(self.SB.at[s, way], self.RB.at[r, way], self.b_send.at[s, way], self.b_recv.at[r, way], to)

    def copy_c(self, k, way):
        s, r = k % N_SC, k % N_RC
        to = self.place.along_first(k % 2, 1 if way == 0 else SIDE - 1)
        return self.remote(self.SC.at[s, way], self.RC.at[r, way], self.c_send.at[s, way], self.c_recv.at[r, way], to)

    def copy_d(self, k, by):
        s, r = k % N_SD, k % N_RD
        to = self.place.along_second(k % 2, by)
        return self.remote(self.SD.at[s, by - 1], self.RD.at[r, by - 1], self.d_send.at[s, by - 1], self.d_recv.at[r, by - 1], to)

    def pair(self, k, target, j):
        odd = k % 2
        x = target + odd * (j - target)
        y = j + odd * (target - j)
        return self.G[k % N_G, x, y, self.place.core].astype(F32) + self.R0[k % N_R0, x, y].astype(F32)

    def stage_a(self, k):
        self.copy_a(k).start()

    def stage_b(self, k):
        a = self.copy_a(k)
        a.wait_recv()
        a.wait_send()
        first, _ = self.place.first(k % 2)
        s = k % N_SB
        for way in range(2):
            for j in range(4):
                far = (j < 2) == (way == 0)
                target = (first + (2 if far else 1 if way == 0 else SIDE - 1)) % SIDE
                self.SB[s, way, j] = self.pair(k, target, j).astype(BF)
            self.copy_b(k, way).start()

    def stage_c(self, k):
        first, _ = self.place.first(k % 2)
        s, r = k % N_SC, k % N_RB
        for way in range(2):
            b = self.copy_b(k, way)
            b.wait_send()
            b.wait_recv()
            target = (first + (1 if way == 0 else SIDE - 1)) % SIDE
            for i in range(2):
                j = i + 2 * way
                self.SC[s, way, i] = (self.pair(k, target, j) + self.RB[r, way, j].astype(F32)).astype(BF)
            self.copy_c(k, way).start()

    def stage_d(self, k):
        for way in range(2):
            c = self.copy_c(k, way)
            c.wait_send()
            c.wait_recv()
        first, second = self.place.first(k % 2)
        b, c = k % N_RB, k % N_RC
        for by in (1, 2, 3, 0):
            j = (second + by) % SIDE
            high = j // 2
            total = self.pair(k, first, j) + self.RC[c, high, j % 2].astype(F32) + self.RB[b, 1 - high, j].astype(F32)
            if by:
                self.SD[k % N_SD, by - 1] = total.astype(BF)
                self.copy_d(k, by).start()
            else:
                self.SO[k % N_SO] = total

    def stage_f(self, k):
        total = self.SO[k % N_SO]
        for by in (1, 2, 3):
            d = self.copy_d(k, by)
            d.wait_send()
            d.wait_recv()
            total = total + self.RD[k % N_RD, by - 1].astype(F32)
        self.finish(k, total.astype(BF))

    def tick(self, t, low, high, load=None):
        for off, stage in ((OFF_F, self.stage_f), (OFF_D, self.stage_d), (OFF_C, self.stage_c), (OFF_B, self.stage_b), (OFF_A, self.stage_a)):
            k = t - off
            if isinstance(k, int):
                if low <= k < high:
                    stage(k)
                continue

            @pl.when(jnp.logical_and(k >= low, k < high))
            def _():
                if off == OFF_A and load is not None:
                    load(k).wait()
                stage(k)


def weights_kernel(shape, *refs):
    d, ff, tokens, own_gu, own_dn, packs = shape
    (aT0, act0, g0, u0, wd, hT, aT1, act1, dgu1, dyT, wg, wu) = refs[:12]
    out, ssq_out, gdn = refs[12:15]
    res, stream, acc, wbuf, stage, ready, ssq, peer = refs[15:23]
    res_sem, stream_sem, acc_sem, w_sem, stage_sem, ready_sem, q_send, q_recv = refs[23:31]
    place = Place()
    tiles = ff // STEP
    half = d // 2
    assert half == STEP
    dn_tile = 4 * own_dn
    dn_tiles = ff // dn_tile
    layer_chunks = 3 * tiles
    assert packs == tiles and packs <= dn_tiles

    place.meet()
    ssq[...] = jnp.zeros_like(ssq)

    def put(k):
        return pltpu.make_async_copy(ready.at[k % 2], out.at[k], ready_sem.at[k % 2])

    def finish(k, g):
        @pl.when(k >= 2)
        def _():
            put(k - 2).wait()

        ready[k % 2] = g
        put(k).start()
        g = g.astype(F32)
        g = g * g
        rows = g[0:8]
        for i in range(8, g.shape[0], 8):
            rows = rows + g[i : i + 8]
        lanes = rows[:, 0:128]
        for i in range(128, g.shape[1], 128):
            lanes = lanes + rows[:, i : i + 128]
        ssq[0] = ssq[0] + lanes

    eng = Reducer(place, refs[31:], finish)

    def copy(src, dst, sem):
        return pltpu.make_async_copy(src, dst, sem)

    def rows(i, size):
        return pl.ds(pl.multiple_of(i * size, 16), size)

    def load_res(which, ref):
        return copy(ref, res.at[which], res_sem.at[which])

    def stream_gu(i, slot):
        return copy(dgu1.at[i], stream.at[slot], stream_sem.at[slot])

    def stream_dn(ref, i, slot):
        return copy(ref.at[rows(i, dn_tile), :], stream.at[slot, pl.ds(0, dn_tile)], stream_sem.at[slot])

    def w_tile(i, part):
        at = pl.ds(pl.multiple_of(i * STEP, 128), STEP)
        return [copy(w.at[1, pl.ds(part * half, half), at], wbuf.at[:, pl.ds(n * STEP, STEP)], w_sem.at[n]) for n, w in enumerate((wg, wu))]

    def hidden_tile(i):
        return [
            copy(g0.at[rows(i, STEP), :], acc.at[pl.ds(0, STEP)], acc_sem.at[0]),
            copy(u0.at[rows(i, STEP), :], acc.at[pl.ds(STEP, STEP)], acc_sem.at[1]),
            copy(wd.at[0, rows(i, STEP), :], wbuf, w_sem.at[0]),
        ]

    def wgrad(which, slot, part, first):
        product = dot(res[which, part * half : (part + 1) * half, :], stream[slot], NT)
        for c in range(2):
            for q in range(SIDE * SIDE):
                x, y, core = part * 2 + q // (2 * SIDE), (q // 2) % SIDE, q % 2
                eng.G[(first + c) % N_G, x, y, core] = product[q * own_gu : (q + 1) * own_gu, c * WIDE : (c + 1) * WIDE].astype(BF)

    stage[...] = jnp.zeros_like(stage)
    full = own_dn // own_gu
    rest = own_dn - full * own_gu
    blocks = d // WIDE

    def out_dn(number, i, s):
        return copy(stage.at[s], gdn.at[number, :, i // 2, pl.ds((i % 2) * 2, 2)], stage_sem.at[s])

    def load_dn(number, chunk, k):
        return copy(gdn.at[number, chunk], eng.G.at[k % N_G], eng.l_sem.at[k % N_G])

    def down_gradient(number, which, i, slot):
        s = i % 2

        @pl.when(i >= 2)
        def _():
            out_dn(number, i - 2, s).wait()

        product = dot(stream[slot, 0:dn_tile, :], res[which], NT)
        for q in range(4):
            for b in range(blocks):
                lanes = slice(b * WIDE, (b + 1) * WIDE)
                for p in range(full):
                    r = q * own_dn + p * own_gu
                    stage[s, p * blocks + b, q // 2, q % 2] = product[r : r + own_gu, lanes].astype(BF)
                r = q * own_dn + full * own_gu
                stage[s, full * blocks + b // 2, q // 2, q % 2, (b % 2) * rest : (b % 2 + 1) * rest] = product[r : r + rest, lanes].astype(BF)
        out_dn(number, i, s).start()

    load_res(1, dyT).start()
    stream_dn(act1, 0, 0).start()
    load_res(0, aT1).start()
    for one in w_tile(0, 0):
        one.start()
    acc[...] = jnp.zeros_like(acc)
    load_res(1, dyT).wait()

    def down1(i, _):
        slot = i % 2
        stream_dn(act1, i, slot).wait()

        @pl.when(i + 1 < dn_tiles)
        def _():
            stream_dn(act1, i + 1, 1 - slot).start()

        @pl.when(i + 1 == dn_tiles)
        def _():
            stream_gu(0, 1 - slot).start()

        down_gradient(0, 1, i, slot)
        return 0

    lax.fori_loop(0, dn_tiles, down1, 0)
    for i in range(dn_tiles - 2, dn_tiles):
        out_dn(0, i, i % 2).wait()
    load_dn(0, 0, 0).start()
    load_res(0, aT1).wait()

    def layer1(i, _):
        slot = (dn_tiles + i) % 2
        load = lambda k: load_dn(0, k // 3, k)
        stream_gu(i, slot).wait()

        @pl.when(i + 1 < tiles)
        def _():
            stream_gu(i + 1, 1 - slot).start()

        @pl.when(i + 1 == tiles)
        def _():
            copy(hT, stream.at[1 - slot], stream_sem.at[1 - slot]).start()

        wgrad(0, slot, 0, 3 * i + 1)
        eng.tick(3 * i, 0, layer_chunks, load)

        @pl.when(i + 1 < tiles)
        def _():
            load(3 * i + 3).start()

        for part in range(2):
            if part:
                wgrad(0, slot, 1, 3 * i + 1)
                eng.tick(3 * i + 1, 0, layer_chunks)
            for one in w_tile(i, part):
                one.wait()
            acc[part * half : (part + 1) * half] += dot(wbuf[...], stream[slot], NN)
            if not part:
                for one in w_tile(i, 1):
                    one.start()

        @pl.when(i + 1 < tiles)
        def _():
            for one in w_tile(i + 1, 0):
                one.start()

        eng.tick(3 * i + 2, 0, layer_chunks)
        return 0

    lax.fori_loop(0, tiles, layer1, 0)

    s_h = (dn_tiles + tiles) % 2
    stream_dn(act0, 0, 1 - s_h).start()
    copy(hT, stream.at[s_h], stream_sem.at[s_h]).wait()

    def back_norm(i, _):
        at = pl.ds(pl.multiple_of(i * 128, 128), 128)
        h = stream[s_h, :, at].astype(F32)
        da = acc[:, at].astype(BF).astype(F32)
        scale = lax.rsqrt(jnp.mean(h * h, 0, keepdims=True) + 1e-6)
        along = jnp.mean(da * h, 0, keepdims=True)
        dh = da * scale - h * (scale * scale * scale * along)
        res[0, :, at] = res[1, :, at] + dh.astype(BF)
        return 0

    lax.fori_loop(0, tokens // 128, back_norm, 0)
    for one in hidden_tile(0):
        one.start()
    load_res(1, aT0).start()

    def down0(i, _):
        slot = (1 - s_h + i) % 2
        stream_dn(act0, i, slot).wait()

        @pl.when(i + 1 < dn_tiles)
        def _():
            stream_dn(act0, i + 1, 1 - slot).start()

        eng.tick(layer_chunks + i, 0, layer_chunks)
        down_gradient(1, 0, i, slot)
        return 0

    assert dn_tiles >= OFF_F
    lax.fori_loop(0, dn_tiles, down0, 0)
    for i in range(dn_tiles - 2, dn_tiles):
        out_dn(1, i, i % 2).wait()
    load_dn(1, 0, layer_chunks).start()
    load_res(1, aT0).wait()

    def layer0(i, _):
        base = layer_chunks + 3 * i
        load = lambda k: load_dn(1, k // 3 - tiles, k)

        @pl.when(i > 0)
        def _():
            eng.tick(base - 2, layer_chunks, 2 * layer_chunks)

        for one in hidden_tile(i):
            one.wait()
        for part in range(2):
            at = pl.ds(part * (tokens // 2), tokens // 2)
            da = dot(wbuf[...], res[0, :, at], NN).astype(BF)
            stream[0, 0:STEP, at], stream[0, STEP:, at] = hidden_back(acc[0:STEP, at], acc[STEP:, at], da)

        @pl.when(i > 0)
        def _():
            eng.tick(base - 1, layer_chunks, 2 * layer_chunks)
            load(base).start()

        @pl.when(i + 1 < tiles)
        def _():
            for one in hidden_tile(i + 1):
                one.start()

        wgrad(1, 0, 0, base + 1)
        eng.tick(base, layer_chunks, 2 * layer_chunks, load)
        wgrad(1, 0, 1, base + 1)
        return 0

    lax.fori_loop(0, tiles, layer0, 0)

    def drain(i, _):
        eng.tick(2 * layer_chunks - 2 + i, layer_chunks, 2 * layer_chunks)
        return 0

    lax.fori_loop(0, 2 + OFF_F, drain, 0)
    for k in range(2 * layer_chunks - 2, 2 * layer_chunks):
        put(k).wait()

    for number, peers in enumerate(([place.other_core()], [place.along_first(0, by) for by in (1, 2, 3)], [place.along_second(0, by) for by in (1, 2, 3)])):
        at = (0, 1, 4)[number]
        copies = []
        for i, to in enumerate(peers):
            copies.append(eng.remote(ssq.at[number], peer.at[at + i], q_send.at[at + i], q_recv.at[at + i], to))
            copies[-1].start()
        total = ssq[number]
        for i, one in enumerate(copies):
            one.wait_recv()
            total = total + peer[at + i]
        for one in copies:
            one.wait_send()
        if number < 2:
            ssq[number + 1] = total
        else:
            ssq_out[...] = total


def weight_gradients(aT0, act0, g0, u0, wd, hT, aT1, act1, dgu1, dyT, wg, wu, n):
    d, tokens = aT0.shape
    ff = act0.shape[0]
    tiles = ff // STEP
    own_gu, own_dn = d // n, ff // n
    blocks = d // WIDE
    full = own_dn // own_gu
    rest = own_dn - full * own_gu
    assert 2 * rest <= own_gu
    packs = full * blocks + -(-blocks // 2)
    dma = pltpu.SemaphoreType.DMA
    flat = (aT0, act0, g0, u0, wd, hT, aT1, act1, dgu1.reshape(tiles, 2 * STEP, tokens), dyT, wg, wu)
    vm = pl.BlockSpec(memory_space=pltpu.VMEM)
    hbm = pl.BlockSpec(memory_space=pl.ANY)
    layer_chunks = 3 * tiles
    out, squares, _ = pl.pallas_call(
        lambda *refs: weights_kernel((d, ff, tokens, own_gu, own_dn, packs), *refs),
        name="weights",
        in_specs=[hbm] * len(flat),
        out_specs=[hbm, vm, hbm],
        out_shape=[
            jax.ShapeDtypeStruct((2 * layer_chunks, own_gu, WIDE), BF),
            jax.ShapeDtypeStruct((8, 128), F32),
            jax.ShapeDtypeStruct((2, packs, SIDE, SIDE, 2, own_gu, WIDE), BF),
        ],
        scratch_shapes=[
            pltpu.VMEM((2, d, tokens), BF),
            pltpu.VMEM((2, 2 * STEP, tokens), BF),
            pltpu.VMEM((d, tokens), F32),
            pltpu.VMEM((STEP, d), BF),
            pltpu.VMEM((2, packs, 2, 2, own_gu, WIDE), BF),
            pltpu.VMEM((2, own_gu, WIDE), BF),
            pltpu.VMEM((3, 8, 128), F32),
            pltpu.VMEM((7, 8, 128), F32),
            dma((2,)),
            dma((2,)),
            dma((2,)),
            dma((2,)),
            dma((2,)),
            dma((2,)),
            dma((7,)),
            dma((7,)),
        ]
        + Reducer.scratch(own_gu, WIDE),
        compiler_params=params(collective_id=1, has_side_effects=True),
        cost_estimate=pl.CostEstimate(flops=18 * d * ff * tokens, bytes_accessed=2**27, transcendentals=0),
    )(*flat)
    layers = []
    for number in (1, 0):
        chunks = out[number * layer_chunks : (number + 1) * layer_chunks].reshape(tiles, 3, own_gu, WIDE)
        dn = chunks[:, 0]
        gu = chunks[:, 1:].transpose(1, 2, 0, 3).reshape(2, own_gu, ff)
        top = dn[: full * blocks].reshape(full, blocks, own_gu, WIDE).transpose(0, 2, 1, 3).reshape(full * own_gu, d)
        low = dn[full * blocks :, : 2 * rest].reshape(-1, rest, WIDE)[:blocks].transpose(1, 0, 2).reshape(rest, d)
        layers.append((gu[0], gu[1], jnp.concatenate([top, low])))
    return [jnp.stack(one) for one in zip(*layers)], jnp.sum(squares)


def gather_kernel(own_ref, out_ref, land, own_sem, out_sem, send, recv):
    place = Place()
    me = place.number(place.x, place.y, place.core)
    mine = pltpu.make_async_copy(own_ref, land.at[:, me], own_sem)
    mine.start()
    place.meet()
    mine.wait()
    started = []

    def at(half, first, second, core=None):
        x, y = (first, second) if half == 0 else (second, first)
        return place.number(place.x + x, place.y + y, place.core if core is None else core)

    def copy(half, number, slot, to):
        strip = land.at[half, number]
        return pltpu.make_async_remote_copy(
            src_ref=strip, dst_ref=strip, send_sem=send.at[half, slot], recv_sem=recv.at[half, slot], device_id={"dp": to}, device_id_type=MESH
        )

    def go(*what):
        started.append(copy(*what))
        started[-1].start()

    def from_side(first, way):
        return 3 + 2 * first + way

    def from_far(first):
        return 11 + first

    def from_core(first, second):
        return 15 + 4 * first + second

    sides = (1, 3)
    for half in range(2):
        for by in (1, 3, 2):
            go(half, me, by - 1, at(half, by, 0))
    for half in range(2):
        for way in range(2):
            go(half, me, from_side(0, way), at(half, 0, sides[way]))
    for half in range(2):
        go(half, me, from_core(0, 0), place.other_core())
    for by in (1, 3, 2):
        for half in range(2):
            first = SIDE - by
            owner = at(half, first, 0)
            copy(half, owner, by - 1, me).wait_recv()
            for way in range(2):
                go(half, owner, from_side(first, way), at(half, 0, sides[way]))
            go(half, owner, from_core(first, 0), place.other_core())
    for first in (0, 3, 1, 2):
        for half in range(2):
            for way in range(2):
                second = SIDE - sides[way]
                owner = at(half, first, second)
                copy(half, owner, from_side(first, way), me).wait_recv()
                if (first < 2) == (way == 0):
                    go(half, owner, from_far(first), at(half, 0, sides[way]))
                go(half, owner, from_core(first, second), place.other_core())
    for first in (0, 3, 1, 2):
        for half in range(2):
            owner = at(half, first, 2)
            copy(half, owner, from_far(first), me).wait_recv()
            go(half, owner, from_core(first, 2), place.other_core())
    for first in range(SIDE):
        for second in range(SIDE):
            for half in range(2):
                copy(half, at(half, first, second, 1 - place.core), from_core(first, second), me).wait_recv()
    outs = []
    each = land.shape[1] // 8
    for i in range(8):
        part = pl.ds(i * each, each)
        outs.append(pltpu.make_async_copy(land.at[:, part], out_ref.at[:, part], out_sem.at[i]))
        outs[-1].start()
    for one in started:
        one.wait_send()
    for one in outs:
        one.wait()


def gather(own, n):
    layers, rows, columns = own.shape
    assert layers == 2
    dma = pltpu.SemaphoreType.DMA
    slots = 15 + SIDE * SIDE
    size = 2 * own.size * n
    out = pl.pallas_call(
        gather_kernel,
        name="gather",
        in_specs=[pl.BlockSpec(memory_space=pl.ANY)],
        out_specs=pl.BlockSpec(memory_space=pl.ANY),
        out_shape=jax.ShapeDtypeStruct((layers, n, rows, columns), BF),
        scratch_shapes=[pltpu.VMEM((layers, n, rows, columns), BF), dma, dma((8,)), dma((2, slots)), dma((2, slots))],
        compiler_params=pltpu.CompilerParams(vmem_limit_bytes=size + 2**21, collective_id=2, has_side_effects=True),
        cost_estimate=pl.CostEstimate(flops=10**11, bytes_accessed=size, transcendentals=0),
    )(own)
    return out.reshape(layers, n * rows, columns)


def settle_kernel(in_ref, out_ref):
    out_ref[...] = in_ref[...]


def settle(w):
    layers, rows, columns = w.shape
    block = pl.BlockSpec((None, 320, columns), lambda i, j: (i, j, 0))
    return pl.pallas_call(
        settle_kernel,
        name="settle",
        grid=(layers, rows // 320),
        in_specs=[block],
        out_specs=block,
        out_shape=jax.ShapeDtypeStruct(w.shape, BF),
        compiler_params=pltpu.CompilerParams(vmem_limit_bytes=2**24),
        cost_estimate=pl.CostEstimate(flops=10**10, bytes_accessed=4 * w.size, transcendentals=0),
    )(w)


def join_kernel(in_ref, out_ref, wide):
    strips, rows, _ = in_ref.shape
    for i in range(strips):
        wide[i * rows : (i + 1) * rows, :] = in_ref[i].astype(F32)
    out_ref[...] = wide[...].astype(BF)


def join(parts):
    n, layers, rows, columns = parts.shape
    size = 4 * rows
    return pl.pallas_call(
        join_kernel,
        name="join",
        grid=(layers, n // 4),
        in_specs=[pl.BlockSpec((4, None, rows, columns), lambda i, j: (j, i, 0, 0))],
        out_specs=pl.BlockSpec((None, size, columns), lambda i, j: (i, j, 0)),
        out_shape=jax.ShapeDtypeStruct((layers, n * rows, columns), BF),
        scratch_shapes=[pltpu.VMEM((size, columns), F32)],
        compiler_params=pltpu.CompilerParams(vmem_limit_bytes=2**24),
        cost_estimate=pl.CostEstimate(flops=10**10, bytes_accessed=4 * parts.size, transcendentals=0),
    )(parts)


def adamw(w, m, v, g):
    m = 0.9 * m + 0.1 * g
    v = 0.95 * v + 0.05 * g * g
    step = m * lax.rsqrt(v + 1e-8) + 0.1 * w
    return (w - 0.02 * step).astype(BF), m, v


def solution(mesh):
    n = mesh.shape["dp"]
    assert n == 2 * SIDE * SIDE and math.isqrt(n // 2) == SIDE

    def one(x, dy, wg, wu, wd, *moments):
        x, dy = x[0], dy[0]
        xT, aT0, g0, u0, act0 = first(0, x, wg, wu)
        hT, aT1 = down(0, wd, act0, xT)
        dyT, act1, dgu1 = last(1, dy, aT1, wg, wu, wd)
        gradients, squares = weight_gradients(aT0, act0, g0, u0, wd, hT, aT1, act1, dgu1, dyT, wg, wu, n)
        count = wg.size + wu.size + wd.size
        factor = jnp.minimum(1.0, 0.5 * lax.rsqrt(squares / count + 1e-30))
        me = lax.axis_index("dp")
        ws, ms, vs = [], [], []
        for w, m, v, g in zip((wg, wu, wd), moments[:3], moments[3:], gradients, strict=True):
            mine = lax.dynamic_slice_in_dim(w, me * m.shape[1], m.shape[1], 1)
            w, m, v = adamw(mine.astype(F32), m, v, g.astype(F32) * factor)
            ws.append(w)
            ms.append(m)
            vs.append(v)
        new_down = join(lax.all_gather(ws[2], "dp", axis=0))
        new_up = settle(lax.all_gather(ws[1], "dp", axis=1, tiled=True))
        new_gate = settle(gather(ws[0], n))
        return (new_gate, new_up, new_down, *ms, *vs)

    seq = P(("rep", "dp"))
    own = P(None, "dp")
    return jax.shard_map(
        one,
        mesh=mesh,
        in_specs=(seq, seq, P(), P(), P()) + (own,) * 6,
        out_specs=(P("rep"),) * 3 + (P("rep", "dp"),) * 6,
        check_vma=False,
    )
```

time: 918 us -> 799 us (0.87)
  waiting for transfers between devices: 215 us -> 49.6 us
  Pallas kernels: 610 us -> 685 us
  local copies, waits for them, and re-layouts: 59.2 us -> 28.4 us
    all_gather x3 -> x2, waiting for transfers between devices: 214 us -> 49.4 us  [the longest x1 49.4 us: one(): new_up = settle(lax.all_gather(ws[1], 'dp', axis=1, tiled=True))]
    pallas_call x3 -> x5, Pallas kernels: 421 us -> 497 us  [the longest x1 346 us: weight_gradients(): pl.pallas_call(lambda *refs: weights_kernel((d, ff, tokens, own_gu, own_d...]
    unnamed x7 -> x28, local copies, waits for them, and re-layouts: 57.8 us -> 23.1 us
  transfers between devices with their start and end apart: 3 -> 2, of which waited for: 3 -> 1; matrix products, arithmetic and copies ran while one was open for 4% -> 2% of each run, Pallas kernels for 0% -> 18%
where the time goes in v2:
time: 799 us; the launch traced here: 791 us
  Pallas kernels  685 us (86%)
  waiting for transfers between devices  49.6 us (6%)
  local copies, waits for them, and re-layouts  28.4 us (4%)
  between operations  15.4 us (2%)
  other arithmetic  12.4 us (2%)
    pallas_call x1, Pallas kernels, weight_gradients(): pl.pallas_call(lambda *refs: weights_kernel((d, ff, tokens, own_gu, own_d...  346 us
    pallas_call x1, Pallas kernels, gather(): pl.pallas_call(gather_kernel, name='gather', in_specs=[pl.BlockSpec(memor...  122 us
    pallas_call x1, Pallas kernels, last(): pl.pallas_call(last_kernel, name='last', grid=(ff // STEP,), in_specs=[wh...  91.1 us
    pallas_call x1, Pallas kernels, first(): pl.pallas_call(first_kernel, name='first', grid=(ff // STEP,), in_specs=[...  63.1 us
    all_gather x1, waiting for transfers between devices, one(): new_up = settle(lax.all_gather(ws[1], 'dp', axis=1, tiled=True))  49.4 us
    pallas_call x1, Pallas kernels, down(): pl.pallas_call(down_kernel, name='down', grid=(tokens // TOK,), in_specs=...  34.2 us
    unnamed x28, local copies, waits for them, and re-layouts  23.1 us
    pallas_call x2, Pallas kernels, settle(): pl.pallas_call(settle_kernel, name='settle', grid=(layers, rows // 320),...  16.1 us
  transfers between devices with their start and end apart: 2, of which 1 were waited for; matrix products, arithmetic and copies ran while one was open for 2% of the time, Pallas kernels for 18%

profile of v2, /device:TPU:97, one launch (start us, length us, event | category | flops | bytes accessed | tf_op | source)
XLA Modules:
  0.0 791.2 jit_solution(400364309890883206)
XLA Ops:
  7.2 0.1 all-gather.6.cloned.1.call-start
  7.3 63.1 %first.1 = (bf16[1280,2048]{1,0:T(8,128)(2,1)}, bf16[1280,2048]{1,0:T(8,128)(2,1)}, f32[4480,2048]{1,0:T(8,128)}, f32[4480,2048]{1,0:T(8,128)}, bf16[4480,2048]{1,0:T(8,128)(2,1)}) custom-call(bf16[2048,1280]{1,0:T(8,128)(2,1)} %bitcast.52, bf16[2,1280,4480]{2,1,0:T(8,128)(2,1)} %refs_10_.1, bf16[2,1280,4480]{2,1,0:T(8,128)(2,1)} %refs_11_.1), custom_call_target="tpu_custom_call" | custom-call | tf_op jit(solution)/shard_map/first/pallas_call | solution.py:68
  70.3 34.2 %down.1 = (bf16[1280,2048]{1,0:T(8,128)(2,1)}, bf16[1280,2048]{1,0:T(8,128)(2,1)}) custom-call(bf16[2,4480,1280]{2,1,0:T(8,128)(2,1)} %refs_4_.1, bf16[4480,2048]{1,0:T(8,128)(2,1)} %get-tuple-element.22.act_ref.refs_1_, bf16[1280,2048]{1,0:T(8,128)(2,1)} %get-tuple-element.25.xT_ref), custom_call_target="tpu_custom_call" | custom-call | tf_op jit(solution)/shard_map/down/pallas_call | solution.py:96
  104.5 91.1 %last.1 = (bf16[1280,2048]{1,0:T(8,128)(2,1)}, bf16[4480,2048]{1,0:T(8,128)(2,1)}, bf16[7,2,640,2048]{3,2,1,0:T(8,128)(2,1)}) custom-call(bf16[2048,1280]{1,0:T(8,128)(2,1)} %bitcast.51, bf16[1280,2048]{1,0:T(8,128)(2,1)} %get-tuple-element.27.aT_ref.refs_6_, bf16[2,1280,4480]{2,1,0:T(8,128)(2,1)} %refs_10_.1, bf16[2,1280,4480]{2,1,0:T(8,128)(2,1)} %refs_11_.1, ...), custom_call_target="tpu_custom_call" | custom-call | tf_op jit(solution)/shard_map/last/pallas_call | solution.py:141
  195.6 345.7 %weights.1 = (bf16[42,40,640]{2,1,0:T(8,128)(2,1)}, f32[8,128]{1,0:T(8,128)}, bf16[2,7,4,4,2,40,640]{6,5,4,3,2,1,0:T(8,128)(2,1)}) custom-call(bf16[1280,2048]{1,0:T(8,128)(2,1)} %get-tuple-element.21.refs_0_, bf16[4480,2048]{1,0:T(8,128)(2,1)} %get-tuple-element.22.act_ref.refs_1_, f32[4480,2048]{1,0:T(8,128)} %get-tuple-element.23.refs_2_, ...), custom_call_target="tpu_custom_call" | custom-call | flops 211392921600 | bytes 134217728 | tf_op jit(solution)/shard_map/weights/pallas_call | solution.py:607
  541.4 1.7 fusion.17
  543.1 0.0 copy-start.2
  543.1 0.0 copy-start.4
  543.2 0.2 copy.55
  543.5 0.0 copy-start.8
  543.5 0.2 copy.57
  543.8 0.3 copy-done.2
  544.1 0.4 copy-done.4
  544.8 0.0 copy-done.8
  544.8 0.6 reduce_sum.9
  546.1 0.1 maximum_bitcast_fusion
  546.1 3.9 fusion.2
  550.0 0.1 all-gather.6.cloned.1.call-update
  550.1 0.1 all-gather.4.cloned.1.call-start
  550.1 1.2 slice_bitcast_fusion.1
  551.3 0.0 copy-start.3
  551.3 0.1 slice_bitcast_fusion.3
  551.4 0.8 copy.64
  552.2 0.5 copy-done.3
  552.7 0.1 slice_bitcast_fusion
  552.8 0.8 slice_bitcast_fusion.2
  553.5 0.8 copy.65
  554.3 4.4 fusion.10
  558.7 0.1 all-gather.4.cloned.1.call-update
  558.8 2.2 copy.60
  561.0 0.0 copy-start.5
  561.0 0.0 copy-start.7
  561.0 2.2 copy.61
  563.2 0.0 copy-start.6
  563.2 0.0 copy-done.5
  563.3 0.0 copy-done.7
  563.3 1.3 copy-done.6
  564.5 3.5 fusion.7
  568.0 121.9 %gather.1 = bf16[2,32,40,4480]{3,2,1,0:T(8,128)(2,1)S(1)} custom-call(bf16[2,40,4480]{2,1,0:T(8,128)(2,1)S(1)} %get-tuple-element.66.own_ref), custom_call_target="tpu_custom_call" | custom-call | flops 99999997952 | bytes 22937600 | tf_op jit(solution)/shard_map/gather/pallas_call | solution.py:735
  690.0 8.1 %settle.2 = bf16[2,1280,4480]{2,1,0:T(8,128)(2,1)} custom-call(bf16[2,1280,4480]{2,1,0:T(8,128)(2,1)S(1)} %bitcast.50), custom_call_target="tpu_custom_call" | custom-call | flops 10000000000 | bytes 45875200 | tf_op jit(solution)/shard_map/settle/pallas_call | solution.py:755
  698.1 0.0 all-gather.6.cloned.1.call-done
  698.1 0.0 copy-start
  698.1 7.7 copy-done
  705.8 13.2 %join.1 = bf16[2,4480,1280]{2,1,0:T(8,128)(2,1)} custom-call(bf16[32,2,140,1280]{3,2,1,0:T(8,128)(2,1)S(1)} %bitcast.49), custom_call_target="tpu_custom_call" | custom-call | flops 10000000000 | bytes 45875200 | tf_op jit(solution)/shard_map/join/pallas_call | solution.py:777
  719.0 49.4 %all-gather.4.cloned.1.call-done.in_ref = bf16[2,1280,4480]{2,1,0:T(8,128)(2,1)} async-done(((bf16[2,40,4480]{2,1,0:T(8,128)(2,1)}), bf16[2,1280,4480]{2,1,0:T(8,128)(2,1)}) %all-gather.4.cloned.1.call-update) | async-done | bytes 22937616 | tf_op jit(solution)/shard_map/all_gather | solution.py:818
  768.4 0.0 copy-start.1
  768.4 7.5 copy-done.1
  775.9 8.0 %settle.3 = bf16[2,1280,4480]{2,1,0:T(8,128)(2,1)} custom-call(bf16[2,1280,4480]{2,1,0:T(8,128)(2,1)S(1)} %copy-done.1), custom_call_target="tpu_custom_call" | custom-call | flops 10000000000 | bytes 45875200 | tf_op jit(solution)/shard_map/settle/pallas_call | solution.py:755
  (16 shorter events, 0.4 us)
Async XLA Ops:
  7.2 690.9 %all-gather.6.cloned.1.call-start = ((), (), s32[]{:S(2)}) async-start(), calls=%async_computation.1 | async-start | bytes 24330240 | tf_op jit(solution)/shard_map/all_gather | solution.py:817
  543.1 1.0 copy-start.2
  543.1 1.3 copy-start.4
  543.5 1.3 copy-start.8
  550.1 218.3 %all-gather.4.cloned.1.call-start = ((), (), s32[]{:S(2)}) async-start(), calls=%async_computation | async-start | bytes 23654400 | tf_op jit(solution)/shard_map/all_gather | solution.py:818
  551.3 1.4 copy-start.3
  561.0 2.2 copy-start.5
  561.0 2.3 copy-start.7
  563.2 1.4 copy-start.6
  698.1 7.7 copy-start
  768.4 7.5 copy-start.1
Sparse Core Ops, SparseCore 0:
  550.2 135.4 all-gather.5
  688.4 79.9 all-gather.3

commit v3 on v2

--- a/solution.py
+++ b/solution.py
@@ -82,14 +82,15 @@
     )(x, w_gate, w_up)
 
 
-def down_kernel(wd_ref, act_ref, xT_ref, hT_ref, aT_ref):
+def down_kernel(wd_ref, act_ref, xT_ref, dy_ref, hT_ref, aT_ref, dyT_ref):
+    dyT_ref[...] = dy_ref[...].astype(F32).T.astype(BF)
     out = dot(wd_ref[...], act_ref[...], TN).astype(BF)
     h = xT_ref[...] + out
     hT_ref[...] = h
     aT_ref[...] = norm_rows(h.astype(F32)).astype(BF)
 
 
-def down(layer, w_down, act, xT):
+def down(layer, w_down, act, xT, dy):
     d, tokens = xT.shape
     ff = act.shape[0]
     column = pl.BlockSpec((d, TOK), lambda i: (0, i))
@@ -101,11 +102,12 @@
             pl.BlockSpec((None, ff, d), lambda i: (layer, 0, 0), pipeline_mode=pl.Buffered(1)),
             pl.BlockSpec((ff, TOK), lambda i: (0, i)),
             column,
+            pl.BlockSpec((TOK, d), lambda i: (i, 0)),
         ],
-        out_specs=[column, column],
-        out_shape=[jax.ShapeDtypeStruct((d, tokens), BF)] * 2,
+        out_specs=[column] * 3,
+        out_shape=[jax.ShapeDtypeStruct((d, tokens), BF)] * 3,
         compiler_params=params(),
-    )(w_down, act, xT)
+    )(w_down, act, xT, dy)
 
 
 def hidden_back(g, u, da):
@@ -115,18 +117,7 @@
     return (da * u * (s + silu * (1.0 - s))).astype(BF), (da * silu).astype(BF)
 
 
-def last_kernel(dy_ref, aT_ref, wg_ref, wu_ref, wd_ref, dyT_ref, act_ref, dgu_ref):
-    tokens = dy_ref.shape[0]
-
-    @pl.when(pl.program_id(0) == 0)
-    def _():
-        def turn(i, _):
-            at = pl.ds(pl.multiple_of(i * 128, 128), 128)
-            dyT_ref[:, at] = dy_ref[at, :].astype(F32).T.astype(BF)
-            return 0
-
-        lax.fori_loop(0, tokens // 128, turn, 0)
-
+def last_kernel(dyT_ref, aT_ref, wg_ref, wu_ref, wd_ref, act_ref, dgu_ref):
     g = dot(wg_ref[...], aT_ref[...], TN)
     u = dot(wu_ref[...], aT_ref[...], TN)
     da = dot(wd_ref[...], dyT_ref[...], NN).astype(BF)
@@ -134,7 +125,7 @@
     dgu_ref[0], dgu_ref[1] = hidden_back(g, u, da)
 
 
-def last(layer, dy, aT, w_gate, w_up, w_down):
+def last(layer, dyT, aT, w_gate, w_up, w_down):
     d, tokens = aT.shape
     ff = w_gate.shape[-1]
     wspec = pl.BlockSpec((None, d, STEP), lambda j: (layer, 0, j))
@@ -142,19 +133,17 @@
         last_kernel,
         name="last",
         grid=(ff // STEP,),
-        in_specs=[whole((tokens, d)), whole((d, tokens)), wspec, wspec, pl.BlockSpec((None, STEP, d), lambda j: (layer, j, 0))],
+        in_specs=[whole((d, tokens)), whole((d, tokens)), wspec, wspec, pl.BlockSpec((None, STEP, d), lambda j: (layer, j, 0))],
         out_specs=[
-            whole((d, tokens)),
             pl.BlockSpec((STEP, tokens), lambda j: (j, 0)),
             pl.BlockSpec((None, 2, STEP, tokens), lambda j: (j, 0, 0, 0)),
         ],
         out_shape=[
-            jax.ShapeDtypeStruct((d, tokens), BF),
             jax.ShapeDtypeStruct((ff, tokens), BF),
             jax.ShapeDtypeStruct((ff // STEP, 2, STEP, tokens), BF),
         ],
         compiler_params=params(),
-    )(dy, aT, w_gate, w_up, w_down)
+    )(dyT, aT, w_gate, w_up, w_down)
 
 
 OFF_A, OFF_B, OFF_C, OFF_D, OFF_F = 0, 1, 3, 5, 7
@@ -324,9 +313,9 @@
 def weights_kernel(shape, *refs):
     d, ff, tokens, own_gu, own_dn, packs = shape
     (aT0, act0, g0, u0, wd, hT, aT1, act1, dgu1, dyT, wg, wu) = refs[:12]
-    out, ssq_out, gdn = refs[12:15]
-    res, stream, acc, wbuf, stage, ready, ssq, peer = refs[15:23]
-    res_sem, stream_sem, acc_sem, w_sem, stage_sem, ready_sem, q_send, q_recv = refs[23:31]
+    out_dn, out_gate, out_up, ssq_out, gdn = refs[12:17]
+    res, stream, acc, wbuf, stage, ready, ssq, peer = refs[17:25]
+    res_sem, stream_sem, acc_sem, w_sem, stage_sem, ready_sem, q_send, q_recv = refs[25:33]
     place = Place()
     tiles = ff // STEP
     half = d // 2
@@ -339,8 +328,11 @@
     place.meet()
     ssq[...] = jnp.zeros_like(ssq)
 
-    def put(k):
-        return pltpu.make_async_copy(ready.at[k % 2], out.at[k], ready_sem.at[k % 2])
+    def put(k, kind=0):
+        layer, i = 1 - k // layer_chunks, (k // 3) % tiles
+        at = pl.ds(pl.multiple_of(i * STEP, 128), STEP)
+        to = out_dn.at[layer, i] if kind == 0 else (out_gate, out_up)[kind - 1].at[layer, :, at]
+        return pltpu.make_async_copy(ready.at[k % 2], to, ready_sem.at[k % 2])
 
     def finish(k, g):
         @pl.when(k >= 2)
@@ -348,7 +340,12 @@
             put(k - 2).wait()
 
         ready[k % 2] = g
-        put(k).start()
+        for kind in range(3):
+
+            @pl.when(k % 3 == kind)
+            def _():
+                put(k, kind).start()
+
         g = g.astype(F32)
         g = g * g
         rows = g[0:8]
@@ -359,7 +356,7 @@
             lanes = lanes + rows[:, i : i + 128]
         ssq[0] = ssq[0] + lanes
 
-    eng = Reducer(place, refs[31:], finish)
+    eng = Reducer(place, refs[33:], finish)
 
     def copy(src, dst, sem):
         return pltpu.make_async_copy(src, dst, sem)
@@ -399,7 +396,7 @@
     rest = own_dn - full * own_gu
     blocks = d // WIDE
 
-    def out_dn(number, i, s):
+    def stage_out(number, i, s):
         return copy(stage.at[s], gdn.at[number, :, i // 2, pl.ds((i % 2) * 2, 2)], stage_sem.at[s])
 
     def load_dn(number, chunk, k):
@@ -410,7 +407,7 @@
 
         @pl.when(i >= 2)
         def _():
-            out_dn(number, i - 2, s).wait()
+            stage_out(number, i - 2, s).wait()
 
         product = dot(stream[slot, 0:dn_tile, :], res[which], NT)
         for q in range(4):
@@ -421,7 +418,7 @@
                     stage[s, p * blocks + b, q // 2, q % 2] = product[r : r + own_gu, lanes].astype(BF)
                 r = q * own_dn + full * own_gu
                 stage[s, full * blocks + b // 2, q // 2, q % 2, (b % 2) * rest : (b % 2 + 1) * rest] = product[r : r + rest, lanes].astype(BF)
-        out_dn(number, i, s).start()
+        stage_out(number, i, s).start()
 
     load_res(1, dyT).start()
     stream_dn(act1, 0, 0).start()
@@ -448,7 +445,7 @@
 
     lax.fori_loop(0, dn_tiles, down1, 0)
     for i in range(dn_tiles - 2, dn_tiles):
-        out_dn(0, i, i % 2).wait()
+        stage_out(0, i, i % 2).wait()
     load_dn(0, 0, 0).start()
     load_res(0, aT1).wait()
 
@@ -527,7 +524,7 @@
     assert dn_tiles >= OFF_F
     lax.fori_loop(0, dn_tiles, down0, 0)
     for i in range(dn_tiles - 2, dn_tiles):
-        out_dn(1, i, i % 2).wait()
+        stage_out(1, i, i % 2).wait()
     load_dn(1, 0, layer_chunks).start()
     load_res(1, aT0).wait()
 
@@ -603,14 +600,15 @@
     flat = (aT0, act0, g0, u0, wd, hT, aT1, act1, dgu1.reshape(tiles, 2 * STEP, tokens), dyT, wg, wu)
     vm = pl.BlockSpec(memory_space=pltpu.VMEM)
     hbm = pl.BlockSpec(memory_space=pl.ANY)
-    layer_chunks = 3 * tiles
-    out, squares, _ = pl.pallas_call(
+    dn, gate, up, squares, _ = pl.pallas_call(
         lambda *refs: weights_kernel((d, ff, tokens, own_gu, own_dn, packs), *refs),
         name="weights",
         in_specs=[hbm] * len(flat),
-        out_specs=[hbm, vm, hbm],
+        out_specs=[hbm, hbm, hbm, vm, hbm],
         out_shape=[
-            jax.ShapeDtypeStruct((2 * layer_chunks, own_gu, WIDE), BF),
+            jax.ShapeDtypeStruct((2, packs, own_gu, WIDE), BF),
+            jax.ShapeDtypeStruct((2, own_gu, ff), BF),
+            jax.ShapeDtypeStruct((2, own_gu, ff), BF),
             jax.ShapeDtypeStruct((8, 128), F32),
             jax.ShapeDtypeStruct((2, packs, SIDE, SIDE, 2, own_gu, WIDE), BF),
         ],
@@ -636,15 +634,9 @@
         compiler_params=params(collective_id=1, has_side_effects=True),
         cost_estimate=pl.CostEstimate(flops=18 * d * ff * tokens, bytes_accessed=2**27, transcendentals=0),
     )(*flat)
-    layers = []
-    for number in (1, 0):
-        chunks = out[number * layer_chunks : (number + 1) * layer_chunks].reshape(tiles, 3, own_gu, WIDE)
-        dn = chunks[:, 0]
-        gu = chunks[:, 1:].transpose(1, 2, 0, 3).reshape(2, own_gu, ff)
-        top = dn[: full * blocks].reshape(full, blocks, own_gu, WIDE).transpose(0, 2, 1, 3).reshape(full * own_gu, d)
-        low = dn[full * blocks :, : 2 * rest].reshape(-1, rest, WIDE)[:blocks].transpose(1, 0, 2).reshape(rest, d)
-        layers.append((gu[0], gu[1], jnp.concatenate([top, low])))
-    return [jnp.stack(one) for one in zip(*layers)], jnp.sum(squares)
+    top = dn[:, : full * blocks].reshape(2, full, blocks, own_gu, WIDE).transpose(0, 1, 3, 2, 4).reshape(2, full * own_gu, d)
+    low = dn[:, full * blocks :, : 2 * rest].reshape(2, -1, rest, WIDE)[:, :blocks].transpose(0, 2, 1, 3).reshape(2, rest, d)
+    return (gate, up, jnp.concatenate([top, low], 1)), jnp.sum(squares)
 
 
 def gather_kernel(own_ref, out_ref, land, own_sem, out_sem, send, recv):
@@ -801,8 +793,8 @@
     def one(x, dy, wg, wu, wd, *moments):
         x, dy = x[0], dy[0]
         xT, aT0, g0, u0, act0 = first(0, x, wg, wu)
-        hT, aT1 = down(0, wd, act0, xT)
-        dyT, act1, dgu1 = last(1, dy, aT1, wg, wu, wd)
+        hT, aT1, dyT = down(0, wd, act0, xT, dy)
+        act1, dgu1 = last(1, dyT, aT1, wg, wu, wd)
         gradients, squares = weight_gradients(aT0, act0, g0, u0, wd, hT, aT1, act1, dgu1, dyT, wg, wu, n)
         count = wg.size + wu.size + wd.size
         factor = jnp.minimum(1.0, 0.5 * lax.rsqrt(squares / count + 1e-30))
@@ -815,8 +807,9 @@
             ms.append(m)
             vs.append(v)
         new_down = join(lax.all_gather(ws[2], "dp", axis=0))
+        new_gate, ms[2], vs[2] = lax.optimization_barrier((gather(ws[0], n), ms[2], vs[2]))
+        new_gate = settle(new_gate)
         new_up = settle(lax.all_gather(ws[1], "dp", axis=1, tiled=True))
-        new_gate = settle(gather(ws[0], n))
         return (new_gate, new_up, new_down, *ms, *vs)
 
     seq = P(("rep", "dp"))

time: 799 us -> 798 us (level)
    unnamed x28 -> x8, local copies, waits for them, and re-layouts: 23.1 us -> 19.6 us
where the time goes in v3:
time: 798 us; the launch traced here: 790 us
  Pallas kernels  681 us (85%)
  waiting for transfers between devices  56.3 us (7%)
  local copies, waits for them, and re-layouts  23.6 us (3%)
  between operations  15 us (2%)
  other arithmetic  13.7 us (2%)
    pallas_call x1, Pallas kernels, weight_gradients(): pl.pallas_call(lambda *refs: weights_kernel((d, ff, tokens, own_gu, own_d...  346 us
    pallas_call x1, Pallas kernels, gather(): pl.pallas_call(gather_kernel, name='gather', in_specs=[pl.BlockSpec(memor...  119 us
    pallas_call x1, Pallas kernels, last(): pl.pallas_call(last_kernel, name='last', grid=(ff // STEP,), in_specs=[wh...  87.9 us
    pallas_call x1, Pallas kernels, first(): pl.pallas_call(first_kernel, name='first', grid=(ff // STEP,), in_specs=[...  63.1 us
    all_gather x1, waiting for transfers between devices, one(): new_up = settle(lax.all_gather(ws[1], 'dp', axis=1, tiled=True))  56.2 us
    pallas_call x1, Pallas kernels, down(): pl.pallas_call(down_kernel, name='down', grid=(tokens // TOK,), in_specs=...  35.7 us
    unnamed x8, local copies, waits for them, and re-layouts  19.6 us
    pallas_call x2, Pallas kernels, settle(): pl.pallas_call(settle_kernel, name='settle', grid=(layers, rows // 320),...  16.1 us
  transfers between devices with their start and end apart: 2, of which 1 were waited for; matrix products, arithmetic and copies ran while one was open for 2% of the time, Pallas kernels for 18%

profile of v3, /device:TPU:97, one launch (start us, length us, event | category | flops | bytes accessed | tf_op | source)
XLA Modules:
  0.0 789.8 jit_solution(1358970384711358659)
XLA Ops:
  7.2 0.1 all-gather.6.cloned.1.call-start
  7.3 63.1 %first.1 = (bf16[1280,2048]{1,0:T(8,128)(2,1)}, bf16[1280,2048]{1,0:T(8,128)(2,1)}, f32[4480,2048]{1,0:T(8,128)}, f32[4480,2048]{1,0:T(8,128)}, bf16[4480,2048]{1,0:T(8,128)(2,1)}) custom-call(bf16[2048,1280]{1,0:T(8,128)(2,1)} %bitcast.13, bf16[2,1280,4480]{2,1,0:T(8,128)(2,1)} %refs_10_.1, bf16[2,1280,4480]{2,1,0:T(8,128)(2,1)} %refs_11_.1), custom_call_target="tpu_custom_call" | custom-call | tf_op jit(solution)/shard_map/first/pallas_call | solution.py:68
  70.3 35.7 %down.1 = (bf16[1280,2048]{1,0:T(8,128)(2,1)}, bf16[1280,2048]{1,0:T(8,128)(2,1)}, bf16[1280,2048]{1,0:T(8,128)(2,1)}) custom-call(bf16[2,4480,1280]{2,1,0:T(8,128)(2,1)} %refs_4_.1, bf16[4480,2048]{1,0:T(8,128)(2,1)} %get-tuple-element.27.act_ref.refs_1_, bf16[1280,2048]{1,0:T(8,128)(2,1)} %get-tuple-element.30.xT_ref, bf16[2048,1280]{1,0:T(8,128)(2,1)} %bitcast.14), custom_call_target="tpu_custom_call" | custom-call | tf_op jit(solution)/shard_map/down/pallas_call | solution.py:97
  106.1 87.9 %last.1 = (bf16[4480,2048]{1,0:T(8,128)(2,1)}, bf16[7,2,640,2048]{3,2,1,0:T(8,128)(2,1)}) custom-call(bf16[1280,2048]{1,0:T(8,128)(2,1)} %get-tuple-element.33.dyT_ref.refs_9_, bf16[1280,2048]{1,0:T(8,128)(2,1)} %get-tuple-element.32.aT_ref.refs_6_, bf16[2,1280,4480]{2,1,0:T(8,128)(2,1)} %refs_10_.1, bf16[2,1280,4480]{2,1,0:T(8,128)(2,1)} %refs_11_.1, ...), custom_call_target="tpu_custom_call" | custom-call | tf_op jit(solution)/shard_map/last/pallas_call | solution.py:132
  194.0 345.9 %weights.1 = (bf16[2,7,40,640]{3,2,1,0:T(8,128)(2,1)}, bf16[2,40,4480]{2,1,0:T(8,128)(2,1)}, bf16[2,40,4480]{2,1,0:T(8,128)(2,1)}, f32[8,128]{1,0:T(8,128)}, bf16[2,7,4,4,2,40,640]{6,5,4,3,2,1,0:T(8,128)(2,1)}) custom-call(bf16[1280,2048]{1,0:T(8,128)(2,1)} %get-tuple-element.26.refs_0_, bf16[4480,2048]{1,0:T(8,128)(2,1)} %get-tuple-element.27.act_ref.refs_1_, ...), custom_call_target="tpu_custom_call" | custom-call | flops 211392921600 | bytes 134217728 | tf_op jit(solution)/shard_map/weights/pallas_call | solution.py:603
  539.9 0.0 copy-start.2
  539.9 1.1 slice.6
  541.0 0.9 slice.7
  541.9 0.0 copy-done.2
  541.9 0.6 reduce_sum.9
  543.2 0.5 copy.34
  543.7 1.2 reshape.39
  544.9 0.1 copy.35
  545.0 0.1 copy.41
  545.1 0.1 reshape.43
  545.2 4.0 fusion.2
  549.2 0.1 all-gather.6.cloned.1.call-update
  549.3 0.1 all-gather.4.cloned.1.call-start
  549.4 4.4 fusion.10
  553.8 0.1 all-gather.4.cloned.1.call-update
  553.8 4.6 fusion.7
  558.4 119.2 %gather.1 = bf16[2,32,40,4480]{3,2,1,0:T(8,128)(2,1)S(1)} custom-call(bf16[2,40,4480]{2,1,0:T(8,128)(2,1)S(1)} %get-tuple-element.58.own_ref), custom_call_target="tpu_custom_call" | custom-call | flops 99999997952 | bytes 22937600 | tf_op jit(solution)/shard_map/gather/pallas_call | solution.py:727
  677.6 2.2 copy.39
  679.8 2.2 copy.40
  682.0 8.0 %settle.2 = bf16[2,1280,4480]{2,1,0:T(8,128)(2,1)} custom-call(bf16[2,1280,4480]{2,1,0:T(8,128)(2,1)S(1)} %bitcast.12), custom_call_target="tpu_custom_call" | custom-call | flops 10000000000 | bytes 45875200 | tf_op jit(solution)/shard_map/settle/pallas_call | solution.py:747
  690.0 0.0 all-gather.6.cloned.1.call-done
  690.0 0.0 copy-start
  690.1 7.7 copy-done
  697.8 13.2 %join.1 = bf16[2,4480,1280]{2,1,0:T(8,128)(2,1)} custom-call(bf16[32,2,140,1280]{3,2,1,0:T(8,128)(2,1)S(1)} %bitcast.11), custom_call_target="tpu_custom_call" | custom-call | flops 10000000000 | bytes 45875200 | tf_op jit(solution)/shard_map/join/pallas_call | solution.py:769
  710.9 56.2 %all-gather.4.cloned.1.call-done.in_ref = bf16[2,1280,4480]{2,1,0:T(8,128)(2,1)} async-done(((bf16[2,40,4480]{2,1,0:T(8,128)(2,1)}), bf16[2,1280,4480]{2,1,0:T(8,128)(2,1)}) %all-gather.4.cloned.1.call-update) | async-done | bytes 22937616 | tf_op jit(solution)/shard_map/all_gather | solution.py:812
  767.2 0.0 copy-start.1
  767.2 7.5 copy-done.1
  774.7 8.0 %settle.3 = bf16[2,1280,4480]{2,1,0:T(8,128)(2,1)} custom-call(bf16[2,1280,4480]{2,1,0:T(8,128)(2,1)S(1)} %copy-done.1), custom_call_target="tpu_custom_call" | custom-call | flops 10000000000 | bytes 45875200 | tf_op jit(solution)/shard_map/settle/pallas_call | solution.py:747
Async XLA Ops:
  7.2 682.9 %all-gather.6.cloned.1.call-start = ((), (), s32[]{:S(2)}) async-start(), calls=%async_computation.1 | async-start | bytes 24330240 | tf_op jit(solution)/shard_map/all_gather | solution.py:809
  539.9 2.1 copy-start.2
  549.3 217.9 %all-gather.4.cloned.1.call-start = ((), (), s32[]{:S(2)}) async-start(), calls=%async_computation | async-start | bytes 23654400 | tf_op jit(solution)/shard_map/all_gather | solution.py:812
  690.0 7.7 copy-start
  767.2 7.5 copy-start.1
Sparse Core Ops, SparseCore 0:
  549.4 134.1 all-gather.5
  686.3 80.8 all-gather.3
